TPU v7x, 256 devices: a whole 4x4x8 slice. The times are simulated.
256 devices in a mesh: ctx: 32 (over z, x_hi, core), cand: 8 (over y, x_lo).
Axes of the slice: x: 4 (x_hi: 2, x_lo: 2; x = x_hi * 2 + x_lo), y: 4, z: 8, core: 2. Of those that a mesh axis runs over, the one named last changes fastest.
Arguments:
- queries: bfloat16 [2048, 1024], P(('cand', 'ctx')), may hold values from -256 to 256
- grad_out: bfloat16 [2048, 1024], P(('cand', 'ctx')), may hold values from -6 to 6
- prefix_keys: bfloat16 [32768, 128], P(('ctx', 'cand')), may hold values from -4 to 4
- prefix_values: bfloat16 [32768, 128], P(('ctx', 'cand')), may hold values from -6 to 6
- cand_keys: bfloat16 [2048, 128], P('cand'), may hold values from -6 to 6
- cand_values: bfloat16 [2048, 128], P('cand'), may hold values from -6 to 6
- lengths: int32 [8, 4], P('cand'), may hold values from 1 to 128, 256 in all within a row
- offsets: int32 [32], P('cand'), may hold values from 8192 to 32768
Outputs:
- grad_queries: bfloat16 [2048, 1024], P(('cand', 'ctx'))
- grad_keys: bfloat16 [32768, 128], P(('ctx', 'cand'))
- grad_values: bfloat16 [32768, 128], P(('ctx', 'cand'))
Inputs may be any that keep to these rules, and one draw needn't show every extreme that they name: Each row of lengths sums to 256.
All inputs are finite; a program needn't handle non-finite values.
Results may differ from a plain program's by a relative error of at most 0.015.
Values may be sent and summed in bfloat16 or wider, within the bound.
A program may use at most 64 MiB of HBM per device.

v0:
```python
import math

import jax
import jax.numpy as jnp
from jax import lax
from jax.sharding import Mesh
from jax.sharding import PartitionSpec as P

HEADS = 8
HD = 128
CAND = ("cand_0", "cand_1")
CAND_CTX = ("cand_0", "cand_1", "ctx")
CTX_CAND = ("ctx", "cand_0", "cand_1")


NEG = -1e30


def side_by_side(arrays, axis, dim, along):
    widths = [a.shape[along] for a in arrays]
    both = jnp.concatenate(arrays, axis=along)
    out = lax.all_gather(both, axis, axis=dim, tiled=True)
    return tuple(jnp.split(out, [sum(widths[:k]) for k in range(1, len(widths))], axis=along))


def sent_to_all(array, axis):
    copies = jnp.broadcast_to(array, (lax.axis_size(axis), *array.shape))
    return lax.all_to_all(copies, axis, split_axis=0, concat_axis=0, tiled=True)


def collected_together(array, axis):
    leaves = jax.tree.leaves(array)
    order = sorted(range(len(leaves)), key=lambda k: -leaves[k].size)
    width = (1, *leaves[order[0]].shape)[-1]
    lines = [
        jnp.pad(leaves[k].reshape(-1), (0, -leaves[k].size % width)).reshape(-1, width)
        for k in order
    ]
    both, at, found = (sent_to_all(jnp.concatenate(lines), axis), 0, {})
    for k, line in zip(order, lines):
        section = both[:, at : at + len(line)].reshape(len(both), -1)
        found[k] = section[:, : leaves[k].size].reshape(-1, *leaves[k].shape)
        at += len(line)
    numbers = iter(range(len(leaves)))
    return jax.tree.map(lambda _: found[next(numbers)], array)


def joined_by_halves(pieces, combine):
    while len(jax.tree.leaves(pieces)[0]) > 1:
        pieces = jax.vmap(combine)(
            *(jax.tree.map(lambda part: part[side::2], pieces) for side in (0, 1))
        )
    return jax.tree.map(lambda part: part[0], pieces)


def merged(array, axis, combine):
    pieces = collected_together(array, axis)
    return joined_by_halves(pieces, combine)


def in_blocks(array, dim, size):
    dims = array.shape
    parts = array.reshape(*dims[:dim], size, dims[dim] // size, *dims[dim + 1 :])
    return jnp.moveaxis(parts, dim, 0)


def sum_at_owner(array, axis, dim):
    parts = in_blocks(array, dim, lax.axis_size(axis))
    arrived = lax.all_to_all(parts, axis, split_axis=0, concat_axis=0, tiled=True)
    return arrived.astype(jnp.float32).sum(axis=0)


def sum_by_axis(terms, axes):
    total = terms.astype(jnp.bfloat16)
    for axis in axes:
        total = lax.psum_scatter(total, axis, scatter_dimension=0, tiled=True)
    return total.astype(jnp.float32)


def spread(weights, values):
    return weights.reshape(weights.shape + (1,) * (values.ndim - 1))


def combine(former, latter):
    highest = jnp.maximum(former[0], latter[0])
    former_weight = jnp.exp(former[0] - highest)
    latter_weight = jnp.exp(latter[0] - highest)
    totals = former[1] * former_weight + latter[1] * latter_weight
    carried = former[2] * spread(former_weight, former[2]) + latter[2] * spread(
        latter_weight, latter[2]
    )
    return (highest, totals, carried)


def body(queries, grad_out, prefix_keys, prefix_values, cand_keys, cand_values, lengths, offsets):
    scaling = 1.0 / math.sqrt(HD)
    owned = queries.shape[0]
    block_len = cand_keys.shape[0]
    ctx_index = lax.axis_index("ctx")
    keys_here, values_here = side_by_side((prefix_keys, prefix_values), CAND, 0, 1)
    key_count = keys_here.shape[0]
    query_block, grad_block = side_by_side((queries, grad_out), "ctx", 0, 1)
    ends = jnp.cumsum(lengths[0])
    tokens_local = jnp.arange(block_len, dtype=jnp.int32)
    segment = jnp.sum((tokens_local[:, None] >= ends[None, :]).astype(jnp.int32), axis=1)
    matches = segment[:, None] == jnp.arange(ends.shape[0], dtype=jnp.int32)[None, :]
    limit = jnp.sum(jnp.where(matches, offsets[None, :], 0), axis=1)
    row_count = block_len * HEADS
    limit_rows = jnp.broadcast_to(limit[:, None], (block_len, HEADS)).reshape(row_count)
    first_key = ctx_index * key_count
    position = first_key + jnp.arange(key_count, dtype=jnp.int32)
    query_rows = query_block.reshape(row_count, HD)
    grad_rows = grad_block.reshape(row_count, HD)
    block_rows = math.gcd(row_count, 512)
    block_total = row_count // block_rows

    def forward_rows(bundle):
        rows_query, rows_grad, rows_limit = bundle
        scores = jnp.dot(rows_query, keys_here.T, preferred_element_type=jnp.float32) * scaling
        visible = position[None, :] < rows_limit[:, None]
        highest = jnp.max(jnp.where(visible, scores, NEG), axis=1)
        expon = jnp.where(visible, jnp.exp(scores - highest[:, None]), 0.0)
        totals = jnp.sum(expon, axis=1)
        products = jnp.dot(rows_grad, values_here.T, preferred_element_type=jnp.float32)
        carried = jnp.sum(expon * products, axis=1)
        return (highest, totals, carried)

    def forward_block(bundle):
        return forward_rows(bundle)

    blocked = (
        query_rows.reshape(block_total, block_rows, HD),
        grad_rows.reshape(block_total, block_rows, HD),
        limit_rows.reshape(block_total, block_rows),
    )
    stat_high, stat_total, stat_carry = lax.map(forward_block, blocked)
    stat_high = stat_high.reshape(row_count)
    stat_total = stat_total.reshape(row_count)
    stat_carry = stat_carry.reshape((row_count,) + stat_carry.shape[2:])
    own_rows = owned * HEADS
    row_start = ctx_index * own_rows
    token_start = ctx_index * owned
    own_query = queries.reshape(own_rows, HD)
    own_grad = grad_out.reshape(own_rows, HD)
    own_tokens = token_start + jnp.arange(owned, dtype=jnp.int32)
    own_segment = lax.dynamic_slice_in_dim(segment, token_start, owned)
    allowed = (own_segment[:, None] == segment[None, :]) & (
        tokens_local[None, :] <= own_tokens[:, None]
    )
    allowed_rows = jnp.broadcast_to(allowed[:, None, :], (owned, HEADS, block_len)).reshape(
        own_rows, block_len
    )
    self_scores = jnp.dot(own_query, cand_keys.T, preferred_element_type=jnp.float32) * scaling
    self_high = jnp.max(jnp.where(allowed_rows, self_scores, NEG), axis=1)
    self_exp = jnp.where(allowed_rows, jnp.exp(self_scores - self_high[:, None]), 0.0)
    self_products = jnp.dot(own_grad, cand_values.T, preferred_element_type=jnp.float32)
    self_carry = jnp.sum(self_exp * self_products, axis=1)
    prefix_own = tuple(
        (
            lax.dynamic_slice_in_dim(whole, row_start, own_rows, 0)
            for whole in (stat_high, stat_total, stat_carry)
        )
    )
    joined = combine(prefix_own, (self_high, jnp.sum(self_exp, axis=1), self_carry))
    stats = tuple(
        (
            lax.dynamic_update_slice_in_dim(whole, piece, row_start, 0)
            for whole, piece in zip((stat_high, stat_total, stat_carry), joined)
        )
    )
    highest, totals, carried = merged(stats, "ctx", combine)
    delta = carried / totals

    def backward_rows(bundle):
        rows_query, rows_grad, rows_limit, rows_high, rows_total, rows_delta = bundle
        scores = jnp.dot(rows_query, keys_here.T, preferred_element_type=jnp.float32) * scaling
        visible = position[None, :] < rows_limit[:, None]
        probs = jnp.where(visible, jnp.exp(scores - rows_high[:, None]), 0.0) / rows_total[:, None]
        products = jnp.dot(rows_grad, values_here.T, preferred_element_type=jnp.float32)
        slopes = (probs * (products - rows_delta[:, None])).astype(jnp.bfloat16)
        return (probs.astype(jnp.bfloat16), slopes)

    def backward_block(bundle):
        return backward_rows(bundle)

    probs_low, slopes = lax.map(
        backward_block,
        blocked
        + (
            highest.reshape(block_total, block_rows),
            totals.reshape(block_total, block_rows),
            delta.reshape(block_total, block_rows),
        ),
    )
    probs_low = probs_low.reshape(row_count, key_count)
    slopes = slopes.reshape(row_count, key_count)
    prefix_grad = sum_at_owner(
        (scaling * jnp.dot(slopes, keys_here, preferred_element_type=jnp.float32))
        .reshape(owned * lax.axis_size("ctx"), HEADS * HD)
        .astype(jnp.bfloat16),
        "ctx",
        0,
    )
    own_high = lax.dynamic_slice_in_dim(highest, row_start, own_rows, 0)
    own_total = lax.dynamic_slice_in_dim(totals, row_start, own_rows, 0)
    own_delta = lax.dynamic_slice_in_dim(delta, row_start, own_rows, 0)
    self_probs = (
        jnp.where(allowed_rows, jnp.exp(self_scores - own_high[:, None]), 0.0) / own_total[:, None]
    )
    self_slopes = (self_probs * (self_products - own_delta[:, None])).astype(jnp.bfloat16)
    self_grad = (
        scaling * jnp.dot(self_slopes, cand_keys, preferred_element_type=jnp.float32)
    ).reshape(owned, HEADS * HD)
    grad_queries = (prefix_grad + self_grad).astype(jnp.bfloat16)
    contract = (((0,), (0,)), ((), ()))
    key_part = scaling * lax.dot_general(
        slopes, query_rows, contract, preferred_element_type=jnp.float32
    )
    value_part = lax.dot_general(probs_low, grad_rows, contract, preferred_element_type=jnp.float32)
    key_value_grads = sum_by_axis(jnp.concatenate([key_part, value_part], axis=1), CAND)
    grad_keys = key_value_grads[:, :HD].astype(jnp.bfloat16)
    grad_values = key_value_grads[:, HD:].astype(jnp.bfloat16)
    return (grad_queries, grad_keys, grad_values)


def solution(mesh):
    torus = Mesh(mesh.devices.reshape(mesh.shape["ctx"], 4, 2), ("ctx", "cand_0", "cand_1"))
    in_specs = (
        P(CAND_CTX, None),
        P(CAND_CTX, None),
        P(CTX_CAND, None),
        P(CTX_CAND, None),
        P(CAND, None),
        P(CAND, None),
        P(CAND, None),
        P(CAND),
    )
    out_specs = (P(CAND_CTX, None), P(CTX_CAND, None), P(CTX_CAND, None))
    return jax.shard_map(body, mesh=torus, in_specs=in_specs, out_specs=out_specs, check_vma=False)
```

profile of v0, /device:TPU:1, one launch (start us, length us, event | category | flops | bytes accessed | tf_op | source)
XLA Modules:
  0.0 212.0 jit_solution(14119434875261860515)
XLA Ops:
  7.2 1.4 pad_maximum_fusion.2
  8.6 0.7 reshape.182
  9.4 0.7 reshape.189
  10.1 0.8 reduce-window.8
  11.1 0.7 select_reduce_fusion
  12.2 0.8 pad_maximum_fusion.1
  13.3 25.6 %all_gather.7 = bf16[1024,256]{1,0:T(8,128)(2,1)S(1)} all-gather(bf16[128,256]{1,0:T(8,128)(2,1)S(1)} %pad_maximum_fusion.1), channel_id=1, replica_groups=mesh['ctx'=32,'cand_0'=4,'cand_1'=2] {'cand_0','cand_1'}, dimensions={0}, use_global_device_ids=true | all-gather | bytes 589824 | tf_op jit(solution)/shard_map/all_gather | solution.py:22
  38.9 1.7 fusion.27
  40.7 52.6 %all-gather.2.cloned.1.call-done = bf16[256,2048]{1,0:T(8,128)(2,1)} async-done(((bf16[8,2048]{1,0:T(8,128)(2,1)}), bf16[256,2048]{1,0:T(8,128)(2,1)}) %all-gather.2.cloned.1.call-update) | async-done | bytes 1048592 | tf_op jit(solution)/shard_map/all_gather | solution.py:22
  93.2 1.3 fusion.48
  95.0 8.9 %while.28 = (s32[]{:T(128)}, f32[4,512]{1,0:T(4,128)S(1)}, f32[4,512]{1,0:T(4,128)S(1)}, f32[4,512]{1,0:T(4,128)S(1)}, s32[4,512]{1,0:T(4,128)S(1)}, /*index=5*/...) while((s32[]{:T(128)}, f32[4,512]{1,0:T(4,128)S(1)}, ...), condition=%wide.region_7.8_spmd.clone, body=%wide.region_3.7_spmd.clone.sunk | while | flops 276299264 | bytes 7127193 | solution.py:136
  95.0 0.6 fusion.77
  95.6 0.8 multiply_reduce_fusion.3
  96.4 0.7 fusion.78
  97.8 0.8 multiply_reduce_fusion.3
  98.6 0.7 fusion.78
  100.0 0.8 multiply_reduce_fusion.3
  100.8 0.7 fusion.78
  102.3 0.8 multiply_reduce_fusion.3
  103.0 0.7 fusion.78
  104.8 1.3 broadcast_in_dim.95
  106.1 5.4 %all-to-all-start = ((f32[32,3,2048]{2,1,0:T(4,128)}), f32[32,3,2048]{2,1,0:T(4,128)S(1)}, u32[]{:S(2)}, u32[]{:S(2)}) async-start(f32[32,3,2048]{2,1,0:T(4,128)} %broadcast_in_dim.95), calls=%async_computation | async-start | bytes 2097152 | tf_op jit(solution)/shard_map/all_to_all | solution.py:28
  111.6 1.0 reshape.198
  112.6 1.1 reshape.196
  113.7 25.9 %all-to-all-done = f32[32,3,2048]{2,1,0:T(4,128)S(1)} async-done(((f32[32,3,2048]{2,1,0:T(4,128)}), f32[32,3,2048]{2,1,0:T(4,128)S(1)}, u32[]{:S(2)}, u32[]{:S(2)}) %all-to-all-start) | async-done | bytes 786464 | tf_op jit(solution)/shard_map/all_to_all | solution.py:28
  142.2 0.7 fusion.43
  142.9 0.7 fusion.45
  143.7 16.5 %while.29 = (s32[]{:T(128)}, bf16[4,512,1024]{2,1,0:T(8,128)(2,1)}, bf16[4,512,1024]{2,1,0:T(8,128)(2,1)}, s32[4,512]{1,0:T(4,128)S(1)}, bf16[4,512,128]{2,1,0:T...) while((s32[]{:T(128)}, bf16[4,512,1024]{2,1,0:T(8,128)(2,1)}, ...), condition=%wide.region_12.13_spmd.clone, body=%wide.region_11.12_spmd.clone.sunk | while | flops 273155072 | bytes 7112853 | solution.py:186
  143.8 2.7 %bitcast_dynamic-update-slice_fusion.2 = (bf16[4,512,1024]{2,1,0:T(8,128)(2,1)}, f32[512,1024]{1,0:T(8,128)S(1)}) fusion(bf16[4,512,1024]{2,1,0:T(8,128)(2,1)} %get-tuple-element.467, s32[]{:T(128)S(6)} %copy.65, f32[512]{0:T(512)S(1)} %bitcast.150, f32[512]{0:T(512)S(1)} %bitcast.151, bf16[1024,128]{1,0:T(8,128)(2,1)S(1)} %get-tuple-element.484, ...), kind=kOutput, calls=%fused_computation.20.clone.1 | convolution fusion | flops 137363456 | bytes 3550208 | tf_op jit(solution)/shard_map/while/body/eval_jaxpr/dot_general | solution.py:176
  146.4 1.4 fusion.82
  147.9 2.7 %bitcast_dynamic-update-slice_fusion.2 = (bf16[4,512,1024]{2,1,0:T(8,128)(2,1)}, f32[512,1024]{1,0:T(8,128)S(1)}) fusion(bf16[4,512,1024]{2,1,0:T(8,128)(2,1)} %get-tuple-element.467, s32[]{:T(128)S(6)} %copy.65, f32[512]{0:T(512)S(1)} %bitcast.150, f32[512]{0:T(512)S(1)} %bitcast.151, bf16[1024,128]{1,0:T(8,128)(2,1)S(1)} %get-tuple-element.484, ...), kind=kOutput, calls=%fused_computation.20.clone.1 | convolution fusion | flops 137363456 | bytes 3550208 | tf_op jit(solution)/shard_map/while/body/eval_jaxpr/dot_general | solution.py:176
  150.6 1.5 fusion.82
  152.1 2.6 %bitcast_dynamic-update-slice_fusion.2 = (bf16[4,512,1024]{2,1,0:T(8,128)(2,1)}, f32[512,1024]{1,0:T(8,128)S(1)}) fusion(bf16[4,512,1024]{2,1,0:T(8,128)(2,1)} %get-tuple-element.467, s32[]{:T(128)S(6)} %copy.65, f32[512]{0:T(512)S(1)} %bitcast.150, f32[512]{0:T(512)S(1)} %bitcast.151, bf16[1024,128]{1,0:T(8,128)(2,1)S(1)} %get-tuple-element.484, ...), kind=kOutput, calls=%fused_computation.20.clone.1 | convolution fusion | flops 137363456 | bytes 3550208 | tf_op jit(solution)/shard_map/while/body/eval_jaxpr/dot_general | solution.py:176
  154.7 1.4 fusion.82
  156.2 2.6 %bitcast_dynamic-update-slice_fusion.2 = (bf16[4,512,1024]{2,1,0:T(8,128)(2,1)}, f32[512,1024]{1,0:T(8,128)S(1)}) fusion(bf16[4,512,1024]{2,1,0:T(8,128)(2,1)} %get-tuple-element.467, s32[]{:T(128)S(6)} %copy.65, f32[512]{0:T(512)S(1)} %bitcast.150, f32[512]{0:T(512)S(1)} %bitcast.151, bf16[1024,128]{1,0:T(8,128)(2,1)S(1)} %get-tuple-element.484, ...), kind=kOutput, calls=%fused_computation.20.clone.1 | convolution fusion | flops 137363456 | bytes 3550208 | tf_op jit(solution)/shard_map/while/body/eval_jaxpr/dot_general | solution.py:176
  158.8 1.4 fusion.82
  160.2 3.1 %fusion.22 = bf16[1024,128]{0,1:T(8,128)(2,1)S(1)} fusion(bf16[2048,1024]{1,0:T(8,128)(2,1)} %bitcast.8, bf16[2048,128]{1,0:T(8,128)(2,1)S(1)} %copy-done.3), kind=kOutput, calls=%fused_computation.35 | convolution fusion | flops 537133056 | bytes 4980736 | tf_op jit(solution)/shard_map/dot_general | solution.py:216
  163.8 0.8 convolution_convert_fusion
  164.6 0.8 pad_maximum_fusion
  165.5 3.4 %fusion.21 = bf16[2048,128]{1,0:T(8,128)(2,1)S(1)} fusion(bf16[2048,1024]{1,0:T(8,128)(2,1)} %bitcast.8, bf16[1024,256]{1,0:T(8,128)(2,1)S(1)} %all_gather.7), kind=kOutput, calls=%fused_computation.33 | convolution fusion | flops 537395200 | bytes 4980736 | tf_op jit(solution)/shard_map/dot_general | solution.py:198
  168.9 1.0 convert_element_type.31
  170.0 5.8 %all-to-all-start.1 = ((bf16[32,8,1024]{2,1,0:T(8,128)(2,1)}), bf16[32,8,1024]{2,1,0:T(8,128)(2,1)S(1)}, u32[]{:S(2)}, u32[]{:S(2)}) async-start(bf16[32,8,1024]{2,1,0:T(8,128)(2,1)} %convert_element_type.31), calls=%async_computation.1 | async-start | bytes 1048576 | tf_op jit(solution)/shard_map/all_to_all | solution.py:69
  176.2 8.6 %reduce-scatter.5.cloned.1.call-done = bf16[256,256]{0,1:T(8,128)(2,1)} async-done(((bf16[1024,256]{0,1:T(8,128)(2,1)}), bf16[256,256]{0,1:T(8,128)(2,1)}) %reduce-scatter.5.cloned.1.call-update) | async-done | bytes 131088 | tf_op jit(solution)/shard_map/reduce_scatter | solution.py:76
  184.7 1.7 copy.23
  186.4 6.2 %all-to-all-done.1 = bf16[32,8,1024]{2,1,0:T(8,128)(2,1)S(1)} async-done(((bf16[32,8,1024]{2,1,0:T(8,128)(2,1)}), bf16[32,8,1024]{2,1,0:T(8,128)(2,1)S(1)}, u32[]{:S(2)}, u32[]{:S(2)}) %all-to-all-start.1) | async-done | bytes 524320 | tf_op jit(solution)/shard_map/all_to_all | solution.py:69
  192.7 0.6 add_convert_fusion
  193.3 10.7 %reduce-scatter.7.cloned.1.call-done = bf16[128,256]{1,0:T(8,128)(2,1)} async-done(((bf16[256,256]{1,0:T(8,128)(2,1)}), bf16[128,256]{1,0:T(8,128)(2,1)}) %reduce-scatter.7.cloned.1.call-update) | async-done | bytes 65552
  204.1 1.4 fusion.50
  (133 shorter events, 8.1 us)
Async XLA Ops:
  7.2 5.9 %copy-start = (bf16[256,128]{1,0:T(8,128)(2,1)S(1)}, bf16[256,128]{1,0:T(8,128)(2,1)}, u32[]{:S(2)}) copy-start(bf16[256,128]{1,0:T(8,128)(2,1)} %param.16) | copy-start | bytes 196612
  7.2 86.1 %all-gather.2.cloned.1.call-start = ((), (), s32[]{:S(2)}) async-start(), calls=%async_computation.4 | async-start | bytes 1081344 | tf_op jit(solution)/shard_map/all_gather | solution.py:22
  103.9 2.2 %copy-start.1 = (bf16[4,512,128]{2,1,0:T(8,128)(2,1)}, bf16[4,512,128]{2,1,0:T(8,128)(2,1)S(1)}, u32[]{:S(2)}) copy-start(bf16[4,512,128]{2,1,0:T(8,128)(2,1)S(1)} %get-tuple-element.502) | copy-start | bytes 1572868
  103.9 2.2 %copy-start.4 = (bf16[1024,128]{1,0:T(8,128)(2,1)}, bf16[1024,128]{1,0:T(8,128)(2,1)S(1)}, u32[]{:S(2)}) copy-start(bf16[1024,128]{1,0:T(8,128)(2,1)S(1)} %get-tuple-element.505) | copy-start | bytes 786436
  106.1 33.5 %all-to-all-start = ((f32[32,3,2048]{2,1,0:T(4,128)}), f32[32,3,2048]{2,1,0:T(4,128)S(1)}, u32[]{:S(2)}, u32[]{:S(2)}) async-start(f32[32,3,2048]{2,1,0:T(4,128)} %broadcast_in_dim.95), calls=%async_computation | async-start | bytes 2097152 | tf_op jit(solution)/shard_map/all_to_all | solution.py:28
  111.6 73.2 %reduce-scatter.5.cloned.1.call-start = ((), (), s32[]{:S(2)}) async-start(), calls=%async_computation.5 | async-start | bytes 655360 | tf_op jit(solution)/shard_map/reduce_scatter | solution.py:76
  140.8 2.9 %copy-start.5 = (bf16[1024,128]{1,0:T(8,128)(2,1)S(1)}, bf16[1024,128]{1,0:T(8,128)(2,1)}, u32[]{:S(2)}) copy-start(bf16[1024,128]{1,0:T(8,128)(2,1)} %copy-done.4) | copy-start | bytes 786436
  143.7 16.5 %copy-start.3 = (bf16[2048,128]{1,0:T(8,128)(2,1)S(1)}, bf16[2048,128]{1,0:T(8,128)(2,1)}, u32[]{:S(2)}) copy-start(bf16[2048,128]{1,0:T(8,128)(2,1)} %reshape.196) | copy-start | bytes 1572868
  160.2 3.1 %copy-start.2 = (bf16[2048,128]{1,0:T(8,128)(2,1)S(1)}, bf16[2048,128]{1,0:T(8,128)(2,1)}, u32[]{:S(2)}) copy-start(bf16[2048,128]{1,0:T(8,128)(2,1)} %reshape.198) | copy-start | bytes 1572868
  160.2 3.6 %copy-start.7 = (bf16[4,512,1024]{2,1,0:T(8,128)(2,1)S(1)}, bf16[4,512,1024]{2,1,0:T(8,128)(2,1)}, u32[]{:S(2)}) copy-start(bf16[4,512,1024]{2,1,0:T(8,128)(2,1)} %get-tuple-element.124) | copy-start | bytes 12582916
  168.9 7.0 %copy-start.6 = (f32[64,256]{1,0:T(8,128)S(1)}, f32[64,256]{1,0:T(8,128)}, u32[]{:S(2)}) copy-start(f32[64,256]{1,0:T(8,128)} %get-tuple-element.269) | copy-start | bytes 196612
  170.0 22.7 %all-to-all-start.1 = ((bf16[32,8,1024]{2,1,0:T(8,128)(2,1)}), bf16[32,8,1024]{2,1,0:T(8,128)(2,1)S(1)}, u32[]{:S(2)}, u32[]{:S(2)}) async-start(bf16[32,8,1024]{2,1,0:T(8,128)(2,1)} %convert_element_type.31), calls=%async_computation.1 | async-start | bytes 1048576 | tf_op jit(solution)/shard_map/all_to_all | solution.py:69
  175.8 28.3 %reduce-scatter.7.cloned.1.call-start = ((), (), s32[]{:S(2)}) async-start(), calls=%async_computation.6 | async-start | bytes 196608
Sparse Core Ops, SparseCore 0:
  11.3 81.8 all-gather.1
  165.6 19.0 reduce-scatter.4
  187.2 16.8 reduce-scatter.6
where the time goes:
time: 213 us; the launch traced here: 212 us
  waiting for transfers between devices  104 us (49%)
  matrix products  31.1 us (15%)
  blocking collectives  25.6 us (12%)
  local copies, waits for them, and re-layouts  15.2 us (7%)
  between operations  14.2 us (7%)
  starting transfers between devices  11.3 us (5%)
  other arithmetic  10.2 us (5%)
    all_gather x1, waiting for transfers between devices, side_by_side(): out = lax.all_gather(both, axis, axis=dim, tiled=True)  52.6 us
    all_to_all x1, waiting for transfers between devices, sent_to_all(): return lax.all_to_all(copies, axis, split_axis=0, concat_axis=0, tiled=True)  25.9 us
    all_gather x1, blocking collectives, side_by_side(): out = lax.all_gather(both, axis, axis=dim, tiled=True)  25.6 us
    unnamed x4, waiting for transfers between devices  10.8 us
    dot_general x4, matrix products, backward_rows(): jnp.dot(rows_query, keys_here.T, preferred_element_type=jnp.float32)  10.5 us
    reduce_scatter x1, waiting for transfers between devices, sum_by_axis(): total = lax.psum_scatter(total, axis, scatter_dimension=0, tiled=True)  8.58 us
    all_to_all x1, waiting for transfers between devices, sum_at_owner(): lax.all_to_all(parts, axis, split_axis=0, concat_axis=0, tiled=True)  6.21 us
    all_to_all x1, starting transfers between devices, sum_at_owner(): lax.all_to_all(parts, axis, split_axis=0, concat_axis=0, tiled=True)  5.83 us
  transfers between devices with their start and end apart: 5, of which 5 were waited for; matrix products, arithmetic and copies ran while one was open for 7% of the time, Pallas kernels for 0%

commit v1 on v0

v1 whole, which is shorter than its diff:
```python
import math

import jax
import jax.numpy as jnp
from jax import lax
from jax.experimental import pallas as pl
from jax.experimental.pallas import tpu as pltpu
from jax.sharding import Mesh
from jax.sharding import PartitionSpec as P

HEADS = 8
HD = 128
NX = NY = 4
NZ = 8
CHIPS = NX * NY
PEERS = 2 * CHIPS
TOK = 8
ROWS = TOK * HEADS
TILE = 4 * ROWS
TILES = PEERS * ROWS // TILE
KEYS = 128
GROUP = 2 * KEYS
GROUPS = NZ * KEYS // GROUP
SAMPLES = 4
AXES = ("z", "xh", "core", "y", "xl")
CAND = ("y", "xl")
CAND_CTX = ("y", "xl", "z", "xh", "core")
CTX_CAND = ("z", "xh", "core", "y", "xl")
MESH = pl.DeviceIdType.MESH
NEG = -1e30
SCALING = 1.0 / math.sqrt(HD)
SCORE = SCALING * math.log2(math.e)
PLACE = {0: 0, 1: 1, 7: 2, 2: 3, 6: 4, 3: 5, 5: 6, 4: 7}
BACK = {place: r for r, place in PLACE.items()}
F32 = jnp.float32
BF16 = jnp.bfloat16
NT = (((1,), (1,)), ((), ()))


def stacked(block):
    wide = block.astype(F32)
    return jnp.concatenate([wide[:, h * HD : (h + 1) * HD] for h in range(HEADS)], axis=0)


def kernel(
    q_ref, g_ref, pk_ref, pv_ref, ck_ref, cv_ref, len_ref, off_ref,
    gq_ref, gk_ref, gv_ref,
    qg, lim, kv, kt, e_buf, p_buf, sl_buf, mg, stat_out, stat_in, fin_out, fin,
    self_e, self_p, dq_out, dq_in, dq_self, part, rs_out, rs_in, rs_end,
    qg_send, qg_recv, lim_send, lim_recv, kv_send, kv_recv,
    st_send, st_recv, fin_send, fin_recv, dq_send, dq_recv,
    rs_send, rs_recv, end_recv,
):
    z, xh, core, y, xl = (lax.axis_index(a) for a in AXES)
    x = 2 * xh + xl
    chip = NY * x + y
    me = 2 * chip + core
    other = 1 - core
    mate = 2 * chip + other
    up = {"z": lax.rem(z + 1, NZ)}
    down = {"z": lax.rem(z + NZ - 1, NZ)}
    near = []
    for dx in range(NX):
        for dy in range(NY):
            if dx or dy:
                px, py = lax.rem(x + dx, NX), lax.rem(y + dy, NY)
                far = min(dx, NX - dx) + min(dy, NY - dy)
                place = {"xh": lax.div(px, 2), "xl": lax.rem(px, 2), "y": py}
                near.append((far, place, NY * px + py))
    near.sort(key=lambda item: item[0])
    sent = []

    def remote(src, dst, send_sem, recv_sem, device):
        return pltpu.make_async_remote_copy(
            src_ref=src, dst_ref=dst, send_sem=send_sem, recv_sem=recv_sem,
            device_id=device, device_id_type=MESH,
        )

    def send(*args):
        copy = remote(*args)
        copy.start()
        sent.append(copy)

    def arrived(dst, send_sem, recv_sem):
        remote(dst, dst, send_sem, recv_sem, {"core": other}).wait_recv()

    qg[me, 0] = stacked(q_ref[...]).astype(BF16)
    qg[me, 1] = stacked(g_ref[...]).astype(BF16)
    kv[0, 0] = pk_ref[...]
    kv[1, 0] = pv_ref[...]

    ends = [len_ref[0, 0]]
    for s in range(1, SAMPLES):
        ends.append(ends[-1] + len_ref[0, s])

    def sample_of(token):
        return sum((token >= end).astype(jnp.int32) for end in ends)

    lane = lax.broadcasted_iota(jnp.int32, (1, 2 * ROWS), 1)
    token = ((z * 2 + xh) * 2 + lax.div(lane, ROWS)) * TOK + lax.rem(lane, TOK)
    sample = sample_of(token)
    limit = jnp.zeros_like(sample)
    for s in range(SAMPLES):
        limit = jnp.where(sample == s, off_ref[s], limit)
    lim[chip] = limit

    barrier = pltpu.get_barrier_semaphore()
    for _, place, _ in near:
        for c in (core, other):
            pl.semaphore_signal(barrier, inc=1, device_id={**place, "core": c}, device_id_type=MESH)
    for place in ({"core": other}, up, down):
        pl.semaphore_signal(barrier, inc=1, device_id=place, device_id_type=MESH)
    pl.semaphore_wait(barrier, PEERS + 1)

    def ring(step):
        for kind in range(2):
            if step <= 4 - kind:
                src, dst = PLACE[step - 1], PLACE[step]
                source = (pk_ref, pv_ref)[kind] if step == 1 else kv.at[kind, src]
                send(source, kv.at[kind, dst], kv_send.at[kind, dst], kv_recv.at[kind, dst], up)
            if step <= 3 + kind:
                src, dst = PLACE[(9 - step) % 8], PLACE[8 - step]
                source = (pk_ref, pv_ref)[kind] if step == 1 else kv.at[kind, src]
                send(source, kv.at[kind, dst], kv_send.at[kind, dst], kv_recv.at[kind, dst], down)

    def ring_wait(step):
        for kind in range(2):
            for r in ([step] if step <= 4 - kind else []) + ([8 - step] if step <= 3 + kind else []):
                arrived(kv.at[kind, PLACE[r]], kv_send.at[kind, PLACE[r]], kv_recv.at[kind, PLACE[r]])

    def rows_wait(slot):
        arrived(qg.at[slot], qg_send.at[0], qg_recv.at[slot])

    def hand_over(slot, number):
        send(qg.at[slot], qg.at[slot], qg_send.at[number], qg_recv.at[slot], {"core": other})

    def plane_wait(far):
        for k, (dist, _, there) in enumerate(near):
            if dist == far:
                rows_wait(2 * there + core)
                hand_over(2 * there + core, CHIPS + k)

    ring(1)
    hand_over(me, 0)
    for k, (_, place, _) in reversed(list(enumerate(near))):
        send(qg.at[me], qg.at[me], qg_send.at[1 + k], qg_recv.at[me], place)
        send(lim.at[chip], lim.at[chip], lim_send.at[k], lim_recv.at[chip], place)

    ring_wait(1)
    ring(2)
    rows_wait(mate)

    own_q = qg[pl.ds(2 * chip, 2), 0].reshape(2 * ROWS, HD)
    own_g = qg[pl.ds(2 * chip, 2), 1].reshape(2 * ROWS, HD)
    block = ck_ref.shape[0]
    cand_token = lax.broadcasted_iota(jnp.int32, (block, 2 * ROWS), 0)
    allowed = (sample_of(cand_token) == sample) & (cand_token <= token)
    score = lax.dot_general(ck_ref[...], own_q, NT, preferred_element_type=F32) * SCORE
    score = jnp.where(allowed, score, NEG)
    own_high = jnp.max(score, axis=0, keepdims=True)
    expon = jnp.exp2(score - own_high)
    product = lax.dot_general(cv_ref[...], own_g, NT, preferred_element_type=F32)
    own_total = jnp.sum(expon, axis=0, keepdims=True)
    own_carry = jnp.sum(expon * product, axis=0, keepdims=True)
    self_e[...] = expon
    self_p[...] = product

    plane_wait(1)
    ring_wait(2)
    ring(3)
    plane_wait(2)
    ring_wait(3)
    ring(4)
    plane_wait(3)
    plane_wait(4)
    for k, (_, _, there) in enumerate(near):
        arrived(lim.at[there], lim_send.at[0], lim_recv.at[there])
    for k, (_, _, there) in enumerate(near):
        rows_wait(2 * there + other)
    ring_wait(4)

    def first_key(place):
        behind = lax.rem(z + NZ - BACK[place], NZ)
        return (((behind * 2 + xh) * 2 + core) * 8 + y * 2 + xl) * KEYS

    starts = [first_key(place) for place in range(NZ)]

    def first_pass(t, _):
        rows_q = qg[pl.ds(4 * t, 4), 0].reshape(TILE, HD)
        rows_g = qg[pl.ds(4 * t, 4), 1].reshape(TILE, HD)
        rows_limit = jnp.concatenate([lim[2 * t], lim[2 * t + 1]], axis=1)
        highs, totals, carries = [], [], []
        for g in range(GROUPS):
            keys = kv[0, 2 * g : 2 * g + 2].reshape(GROUP, HD)
            values = kv[1, 2 * g : 2 * g + 2].reshape(GROUP, HD)
            score = lax.dot_general(keys, rows_q, NT, preferred_element_type=F32) * SCORE
            index = lax.broadcasted_iota(jnp.int32, (KEYS, TILE), 0)
            seen = [index < rows_limit - starts[2 * g + i] for i in range(2)]
            score = jnp.concatenate(
                [jnp.where(seen[i], score[i * KEYS : (i + 1) * KEYS], NEG) for i in range(2)], axis=0
            )
            high = jnp.max(score, axis=0, keepdims=True)
            expon = jnp.exp2(score - high)
            product = lax.dot_general(values, rows_g, NT, preferred_element_type=F32)
            e_buf[t, g * GROUP : (g + 1) * GROUP] = expon
            p_buf[t, g * GROUP : (g + 1) * GROUP] = product
            highs.append(high)
            totals.append(jnp.sum(expon, axis=0, keepdims=True))
            carries.append(jnp.sum(expon * product, axis=0, keepdims=True))
        top = highs[0]
        for g in range(1, GROUPS):
            top = jnp.maximum(top, highs[g])
        total, carry = jnp.zeros_like(top), jnp.zeros_like(top)
        for g in range(GROUPS):
            weight = jnp.exp2(highs[g] - top)
            total += totals[g] * weight
            carry += carries[g] * weight
        mg[t] = jnp.concatenate(highs, axis=0)
        stats = jnp.concatenate([top, total, carry, top], axis=0)
        stat_out[2 * t] = stats[:, : 2 * ROWS]
        stat_out[2 * t + 1] = stats[:, 2 * ROWS :]
        return 0

    lax.fori_loop(0, TILES, first_pass, 0)

    for k, (_, place, there) in reversed(list(enumerate(near))):
        for i, c in enumerate((core, other)):
            send(
                stat_out.at[there], stat_in.at[me], st_send.at[2 * k + i], st_recv.at[me],
                {**place, "core": c},
            )
    send(stat_out.at[chip], stat_in.at[me], st_send.at[PEERS - 2], st_recv.at[me], {"core": other})
    stat_in[me] = stat_out[chip]
    for place in range(NZ):
        kt[:, place * KEYS : (place + 1) * KEYS] = kv[0, place].astype(F32).T.astype(BF16)
    arrived(stat_in.at[mate], st_send.at[0], st_recv.at[mate])
    for _, _, there in near:
        for c in (core, other):
            arrived(stat_in.at[2 * there + c], st_send.at[0], st_recv.at[2 * there + c])
    top = own_high
    for i in range(PEERS):
        top = jnp.maximum(top, stat_in[i][0:1])
    weight = jnp.exp2(own_high - top)
    total, carry = own_total * weight, own_carry * weight
    for i in range(PEERS):
        stats = stat_in[i]
        weight = jnp.exp2(stats[0:1] - top)
        total += stats[1:2] * weight
        carry += stats[2:3] * weight
    inverse = 1.0 / total
    delta = carry * inverse
    final = jnp.concatenate([top, inverse, delta, top], axis=0)
    fin_out[...] = final
    fin[chip] = final
    for k, (_, place, _) in reversed(list(enumerate(near))):
        send(fin_out, fin.at[chip], fin_send.at[k], fin_recv.at[chip], place)

    self_probs = self_e[...] * (jnp.exp2(own_high - top) * inverse)
    self_slopes = (self_probs * (self_p[...] - delta)).astype(BF16)
    self_keys = ck_ref[...].astype(F32).T.astype(BF16)
    dq_self[...] = (jnp.dot(self_keys, self_slopes, preferred_element_type=F32) * SCALING).T

    for _, _, there in near:
        arrived(fin.at[there], fin_send.at[0], fin_recv.at[there])

    def second_pass(place, _):
        g = lax.div(place, 2)
        grad_k = jnp.zeros((KEYS, HD), F32)
        grad_v = jnp.zeros((KEYS, HD), F32)
        for t in range(TILES):
            final = jnp.concatenate([fin[2 * t], fin[2 * t + 1]], axis=1)
            weight = jnp.exp2(mg[t, pl.ds(g, 1)] - final[0:1]) * final[1:2]
            at = pl.ds(pl.multiple_of(place * KEYS, KEYS), KEYS)
            probs = e_buf[t, at] * weight
            slopes = (probs * (p_buf[t, at] - final[2:3])).astype(BF16)
            sl_buf[t, at] = slopes
            rows_q = qg[4 * t : 4 * t + 4, 0].reshape(TILE, HD)
            rows_g = qg[4 * t : 4 * t + 4, 1].reshape(TILE, HD)
            grad_v += jnp.dot(probs.astype(BF16), rows_g, preferred_element_type=F32)
            grad_k += jnp.dot(slopes, rows_q, preferred_element_type=F32)
        part[place, 0] = grad_k * SCALING
        part[place, 1] = grad_v
        return 0

    def pass_on(back, kind, first):
        place = PLACE[back]
        total = part[place, kind]
        if not first:
            arrived(rs_in.at[kind, place], rs_send.at[kind, place], rs_recv.at[kind, place])
            total = total + rs_in[kind, place].astype(F32)
        rs_out[kind, place] = total.astype(BF16)
        going_down = back < 4 or (back == 4 and kind == 0)
        nearer = back - 1 if going_down else (back + 1) % 8
        way = 0 if going_down else 1
        if nearer:
            dst, sem = rs_in.at[kind, PLACE[nearer]], rs_recv.at[kind, PLACE[nearer]]
        else:
            dst, sem = rs_end.at[kind, way], end_recv.at[kind, way]
        send(rs_out.at[kind, place], dst, rs_send.at[kind, place], sem, down if going_down else up)

    second_pass(7, 0)
    pass_on(4, 0, True)
    pass_on(4, 1, True)
    lax.fori_loop(0, 4, lambda i, c: second_pass(6 - i, c), 0)
    pass_on(5, 0, True)
    pass_on(3, 1, True)
    pass_on(3, 0, False)
    pass_on(5, 1, False)
    lax.fori_loop(0, 3, lambda i, c: second_pass(2 - i, c), 0)
    for back in (2, 6):
        for kind in range(2):
            pass_on(back, kind, False)

    def query_pass(t, _):
        grads = jnp.dot(kt[...], sl_buf[t], preferred_element_type=F32) * SCALING
        dq_out[pl.ds(4 * t, 4)] = grads.T.astype(BF16).reshape(4, ROWS, HD)
        return 0

    lax.fori_loop(0, TILES, query_pass, 0)
    for k, (_, place, there) in reversed(list(enumerate(near))):
        for i, c in enumerate((core, other)):
            send(
                dq_out.at[2 * there + c], dq_in.at[me], dq_send.at[2 * k + i], dq_recv.at[me],
                {**place, "core": c},
            )
    send(dq_out.at[mate], dq_in.at[me], dq_send.at[PEERS - 2], dq_recv.at[me], {"core": other})
    dq_in[me] = dq_out[me]
    for back in (1, 7):
        for kind in range(2):
            pass_on(back, kind, False)
    arrived(dq_in.at[mate], dq_send.at[0], dq_recv.at[mate])
    for _, _, there in near:
        for c in (core, other):
            arrived(dq_in.at[2 * there + c], dq_send.at[0], dq_recv.at[2 * there + c])
    grads = dq_self[pl.ds(pl.multiple_of(core * ROWS, ROWS), ROWS)]
    for i in range(PEERS):
        grads += dq_in[i].astype(F32)
    gq_ref[...] = jnp.concatenate(
        [grads[h * TOK : (h + 1) * TOK] for h in range(HEADS)], axis=1
    ).astype(BF16)
    for kind, out in enumerate((gk_ref, gv_ref)):
        total = part[0, kind]
        for way in range(2):
            arrived(rs_end.at[kind, way], rs_send.at[kind, 0], end_recv.at[kind, way])
            total = total + rs_end[kind, way].astype(F32)
        out[...] = total.astype(BF16)
    for copy in sent:
        copy.wait_send()


def body(queries, grad_out, prefix_keys, prefix_values, cand_keys, cand_values, lengths, offsets):
    vmem = pl.BlockSpec(memory_space=pltpu.VMEM)
    smem = pl.BlockSpec(memory_space=pltpu.SMEM)
    keys = NZ * KEYS
    block = cand_keys.shape[0]
    sem = pltpu.SemaphoreType.DMA
    return pl.pallas_call(
        kernel,
        out_shape=(
            jax.ShapeDtypeStruct(queries.shape, BF16),
            jax.ShapeDtypeStruct(prefix_keys.shape, BF16),
            jax.ShapeDtypeStruct(prefix_values.shape, BF16),
        ),
        in_specs=[vmem] * 6 + [smem] * 2,
        out_specs=(vmem,) * 3,
        scratch_shapes=[
            pltpu.VMEM((PEERS, 2, ROWS, HD), BF16),
            pltpu.VMEM((CHIPS, 1, 2 * ROWS), jnp.int32),
            pltpu.VMEM((2, NZ, KEYS, HD), BF16),
            pltpu.VMEM((HD, keys), BF16),
            pltpu.VMEM((TILES, keys, TILE), F32),
            pltpu.VMEM((TILES, keys, TILE), F32),
            pltpu.VMEM((TILES, keys, TILE), BF16),
            pltpu.VMEM((TILES, GROUPS, TILE), F32),
            pltpu.VMEM((CHIPS, 4, 2 * ROWS), F32),
            pltpu.VMEM((PEERS, 4, 2 * ROWS), F32),
            pltpu.VMEM((4, 2 * ROWS), F32),
            pltpu.VMEM((CHIPS, 4, 2 * ROWS), F32),
            pltpu.VMEM((block, 2 * ROWS), F32),
            pltpu.VMEM((block, 2 * ROWS), F32),
            pltpu.VMEM((PEERS, ROWS, HD), BF16),
            pltpu.VMEM((PEERS, ROWS, HD), BF16),
            pltpu.VMEM((2 * ROWS, HD), F32),
            pltpu.VMEM((NZ, 2, KEYS, HD), F32),
            pltpu.VMEM((2, NZ, KEYS, HD), BF16),
            pltpu.VMEM((2, NZ, KEYS, HD), BF16),
            pltpu.VMEM((2, 2, KEYS, HD), BF16),
            sem((PEERS - 1,)),
            sem((PEERS,)),
            sem((CHIPS - 1,)),
            sem((CHIPS,)),
            sem((2, NZ)),
            sem((2, NZ)),
            sem((PEERS - 1,)),
            sem((PEERS,)),
            sem((CHIPS - 1,)),
            sem((CHIPS,)),
            sem((PEERS - 1,)),
            sem((PEERS,)),
            sem((2, NZ)),
            sem((2, NZ)),
            sem((2, 2)),
        ],
        compiler_params=pltpu.CompilerParams(
            collective_id=0, has_side_effects=True, vmem_limit_bytes=56 * 1024 * 1024
        ),
        name="attention_grads",
    )(queries, grad_out, prefix_keys, prefix_values, cand_keys, cand_values, lengths, offsets)


def solution(mesh):
    torus = Mesh(mesh.devices.reshape(NZ, 2, 2, NY, 2), AXES)
    in_specs = (
        P(CAND_CTX, None),
        P(CAND_CTX, None),
        P(CTX_CAND, None),
        P(CTX_CAND, None),
        P(CAND, None),
        P(CAND, None),
        P(CAND, None),
        P(CAND),
    )
    out_specs = (P(CAND_CTX, None), P(CTX_CAND, None), P(CTX_CAND, None))
    return jax.shard_map(body, mesh=torus, in_specs=in_specs, out_specs=out_specs, check_vma=False)
```

time: 213 us -> 65.4 us (0.31)
  waiting for transfers between devices: 104 us -> 0 us
  Pallas kernels: 0 us -> 61.8 us
  matrix products: 31.1 us -> 0 us
  blocking collectives: 25.6 us -> 0 us
  between operations: 14.2 us -> 0.65 us
  local copies, waits for them, and re-layouts: 15.2 us -> 2.72 us
  starting transfers between devices: 11.3 us -> 0 us
  other arithmetic: 10.2 us -> 0 us
    pallas_call x0 -> x1, Pallas kernels: none -> 61.8 us  [body(): pl.pallas_call(kernel, out_shape=(jax.ShapeDtypeStruct(queries.shape, BF1...]
    all_gather x1 -> x0, waiting for transfers between devices: 52.6 us -> none  [side_by_side(): out = lax.all_gather(both, axis, axis=dim, tiled=True)]
    all_to_all x2 -> x0, waiting for transfers between devices: 32.2 us -> none  [the longest x1 25.9 us: sent_to_all(): return lax.all_to_all(copies, axis, split_axis=0, concat_axis=0, tiled=True)]
    dot_general x22 -> x0, matrix products: 31.1 us -> none  [the longest x4 10.5 us: backward_rows(): jnp.dot(rows_query, keys_here.T, preferred_element_type=jnp.float32)]
    all_gather x1 -> x0, blocking collectives: 25.6 us -> none  [side_by_side(): out = lax.all_gather(both, axis, axis=dim, tiled=True)]
    all_to_all x2 -> x0, starting transfers between devices: 11.2 us -> none  [the longest x1 5.83 us: sum_at_owner(): lax.all_to_all(parts, axis, split_axis=0, concat_axis=0, tiled=True)]
    unnamed x4 -> x0, waiting for transfers between devices: 10.8 us -> none
    reduce_scatter x1 -> x0, waiting for transfers between devices: 8.58 us -> none  [sum_by_axis(): total = lax.psum_scatter(total, axis, scatter_dimension=0, tiled=True)]
  transfers between devices with their start and end apart: 5 -> 0, of which waited for: 5 -> 0; matrix products, arithmetic and copies ran while one was open for 7% -> 0% of each run, Pallas kernels for 0% -> 0%
where the time goes in v1:
time: 65.4 us; the launch traced here: 65.1 us
  Pallas kernels  61.8 us (94%)
  local copies, waits for them, and re-layouts  2.72 us (4%)
    pallas_call x1, Pallas kernels, body(): pl.pallas_call(kernel, out_shape=(jax.ShapeDtypeStruct(queries.shape, BF1...  61.8 us
    unnamed x7, local copies, waits for them, and re-layouts  2.72 us

profile of v1, /device:TPU:1, one launch (start us, length us, event | category | flops | bytes accessed | tf_op | source)
XLA Modules:
  0.0 65.1 jit_solution(9714647191581092563)
XLA Ops:
  0.6 61.8 %attention_grads.1 = (bf16[8,1024]{1,0:T(8,128)(2,1)}, bf16[128,128]{1,0:T(8,128)(2,1)}, bf16[128,128]{1,0:T(8,128)(2,1)}) custom-call(bf16[8,1024]{1,0:T(8,128)(2,1)} %q_ref.1, bf16[8,1024]{1,0:T(8,128)(2,1)} %g_ref.1, bf16[128,128]{1,0:T(8,128)(2,1)} %pk_ref.1, bf16[128,128]{1,0:T(8,128)(2,1)} %pv_ref.1, bf16[256,128]{1,0:T(8,128)(2,1)} %ck_ref.1, ...), custom_call_target="tpu_custom_call" | custom-call | tf_op jit(solution)/shard_map/attention_grads/pallas_call | solution.py:357
  62.4 0.0 copy-start.1
  62.4 1.3 %copy.14 = bf16[8,1024]{1,0:T(8,128)(2,1)} copy(bf16[8,1024]{1,0:T(8,128)(2,1)} %get-tuple-element.6) | data formatting | bytes 32768
  63.8 0.0 copy-done.1
  63.8 0.0 copy-start
  63.8 0.6 copy.15
  64.4 0.2 copy-done
  64.5 0.6 copy.16
Async XLA Ops:
  62.4 1.3 %copy-start.1 = (bf16[128,128]{1,0:T(8,128)(2,1)S(1)}, bf16[128,128]{1,0:T(8,128)(2,1)}, u32[]{:S(2)}) copy-start(bf16[128,128]{1,0:T(8,128)(2,1)} %get-tuple-element.7) | copy-start | bytes 98308
  63.8 0.8 %copy-start = (bf16[128,128]{1,0:T(8,128)(2,1)S(1)}, bf16[128,128]{1,0:T(8,128)(2,1)}, u32[]{:S(2)}) copy-start(bf16[128,128]{1,0:T(8,128)(2,1)} %get-tuple-element.8) | copy-start | bytes 98308

commit v2 on v1

v2 whole, which is shorter than its diff:
```python
import math

import jax
import jax.numpy as jnp
from jax import lax
from jax.experimental import pallas as pl
from jax.experimental.pallas import tpu as pltpu
from jax.sharding import Mesh
from jax.sharding import PartitionSpec as P

HEADS = 8
HD = 128
NX = NY = 4
NZ = 8
CHIPS = NX * NY
PEERS = 2 * CHIPS
TOK = 8
ROWS = TOK * HEADS
TILE = 4 * ROWS
TILES = PEERS * ROWS // TILE
KEYS = 128
GROUPS = ((0, 2), (2, 5), (5, 8))
SAMPLES = 4
AXES = ("z", "xh", "core", "y", "xl")
CAND = ("y", "xl")
CAND_CTX = ("y", "xl", "z", "xh", "core")
CTX_CAND = ("z", "xh", "core", "y", "xl")
MESH = pl.DeviceIdType.MESH
NEG = -1e30
SCALING = 1.0 / math.sqrt(HD)
SCORE = SCALING * math.log2(math.e)
PLACE = {0: 0, 1: 1, 7: 2, 2: 3, 6: 4, 3: 5, 5: 6, 4: 7}
BACK = {place: r for r, place in PLACE.items()}
OFFSETS = sorted(
    ((dx, dy) for dx in range(NX) for dy in range(NY)),
    key=lambda o: min(o[0], NX - o[0]) + min(o[1], NY - o[1]),
)
FAR = [min(dx, NX - dx) + min(dy, NY - dy) for dx, dy in OFFSETS]
SEEN = [OFFSETS.index(((NX - dx) % NX, (NY - dy) % NY)) for dx, dy in OFFSETS]
F32 = jnp.float32
BF16 = jnp.bfloat16
NT = (((1,), (1,)), ((), ()))


def stacked(block):
    wide = block.astype(F32)
    return jnp.concatenate([wide[:, h * HD : (h + 1) * HD] for h in range(HEADS)], axis=0)


def kernel(
    q_ref, g_ref, pk_ref, pv_ref, ck_ref, cv_ref, len_ref, off_ref,
    gq_ref, gk_ref, gv_ref,
    qg, lim, kv, kt, e_buf, p_buf, mg, tot, car, loc, ab, stat_out, stat_in, fin_out, fin,
    self_e, self_p, dq_out, dq_mate, dq_sum, dq_in, dq_self, part, rs_out, rs_near, rs_far, rs_end,
    qg_send, qg_recv, lim_send, lim_recv, kv_send, kv_recv,
    st_send, st_recv, fin_send, fin_recv, mate_send, mate_recv, dq_send, dq_recv,
    rs_send, near_recv, far_recv, end_recv,
):
    z, xh, core, y, xl = (lax.axis_index(a) for a in AXES)
    x = 2 * xh + xl
    other = 1 - core
    mate = {"core": other}
    up, up2, down2, down = ({"z": lax.rem(z + d, NZ)} for d in (1, 2, NZ - 2, NZ - 1))
    chips = []
    for dx, dy in OFFSETS:
        px, py = lax.rem(x + dx, NX), lax.rem(y + dy, NY)
        chips.append({"xh": lax.div(px, 2), "xl": lax.rem(px, 2), "y": py})
    nearest = list(range(1, CHIPS))
    farthest = nearest[::-1]
    sent = []

    def remote(src, dst, send_sem, recv_sem, device):
        return pltpu.make_async_remote_copy(
            src_ref=src, dst_ref=dst, send_sem=send_sem, recv_sem=recv_sem,
            device_id=device, device_id_type=MESH,
        )

    def send(*args):
        copy = remote(*args)
        copy.start()
        sent.append(copy)

    def arrived(dst, send_sem, recv_sem):
        remote(dst, dst, send_sem, recv_sem, mate).wait_recv()

    qg[core, 0] = stacked(q_ref[...]).astype(BF16)
    qg[core, 1] = stacked(g_ref[...]).astype(BF16)
    kv[0, 0] = pk_ref[...]
    kv[1, 0] = pv_ref[...]

    ends = [len_ref[0, 0]]
    for s in range(1, SAMPLES):
        ends.append(ends[-1] + len_ref[0, s])

    def sample_of(token):
        return sum((token >= end).astype(jnp.int32) for end in ends)

    lane = lax.broadcasted_iota(jnp.int32, (1, 2 * ROWS), 1)
    token = ((z * 2 + xh) * 2 + lax.div(lane, ROWS)) * TOK + lax.rem(lane, TOK)
    sample = sample_of(token)
    limit = jnp.zeros_like(sample)
    for s in range(SAMPLES):
        limit = jnp.where(sample == s, off_ref[s], limit)
    lim[0] = limit

    barrier = pltpu.get_barrier_semaphore()
    for r in nearest:
        for c in (core, other):
            pl.semaphore_signal(
                barrier, inc=1, device_id={**chips[r], "core": c}, device_id_type=MESH
            )
    for device in (mate, up, down, up2, down2):
        pl.semaphore_signal(barrier, inc=1, device_id=device, device_id_type=MESH)
    pl.semaphore_wait(barrier, PEERS + 3)

    def kv_to(kind, back, new_back, device):
        src = (pk_ref, pv_ref)[kind] if back == 0 else kv.at[kind, PLACE[back]]
        at = PLACE[new_back]
        send(src, kv.at[kind, at], kv_send.at[kind, at], kv_recv.at[kind, at], device)

    def kv_wait(kind, back):
        at = PLACE[back]
        arrived(kv.at[kind, at], kv_send.at[kind, at], kv_recv.at[kind, at])

    def rows_wait(slot):
        arrived(qg.at[slot], qg_send.at[0], qg_recv.at[slot])

    def hand_over(r):
        slot = 2 * r + core
        send(qg.at[slot], qg.at[slot], qg_send.at[r], qg_recv.at[slot], mate)

    def plane_wait(far):
        for r in nearest:
            if FAR[r] == far:
                rows_wait(2 * r + core)
                hand_over(r)

    for kind in range(2):
        kv_to(kind, 0, 2, up2)
        kv_to(kind, 0, 6, down2)
    hand_over(0)
    for r in farthest:
        slot = 2 * SEEN[r] + core
        send(qg.at[core], qg.at[slot], qg_send.at[CHIPS - 1 + r], qg_recv.at[slot], chips[r])
    for kind in range(2):
        kv_to(kind, 0, 1, up)
        kv_to(kind, 0, 7, down)
    for r in farthest:
        send(lim.at[0], lim.at[SEEN[r]], lim_send.at[r], lim_recv.at[SEEN[r]], chips[r])

    rows_wait(other)
    own_q = qg[0:2, 0].reshape(2 * ROWS, HD)
    own_g = qg[0:2, 1].reshape(2 * ROWS, HD)
    block = ck_ref.shape[0]
    cand_token = lax.broadcasted_iota(jnp.int32, (block, 2 * ROWS), 0)
    allowed = (sample_of(cand_token) == sample) & (cand_token <= token)
    score = lax.dot_general(ck_ref[...], own_q, NT, preferred_element_type=F32) * SCORE
    score = jnp.where(allowed, score, NEG)
    own_high = jnp.max(score, axis=0, keepdims=True)
    expon = jnp.exp2(score - own_high)
    product = lax.dot_general(cv_ref[...], own_g, NT, preferred_element_type=F32)
    own_total = jnp.sum(expon, axis=0, keepdims=True)
    own_carry = jnp.sum(expon * product, axis=0, keepdims=True)
    self_e[...] = expon
    self_p[...] = product

    def first_key(place):
        behind = lax.rem(z + NZ - BACK[place], NZ)
        return (((behind * 2 + xh) * 2 + core) * 8 + y * 2 + xl) * KEYS

    starts = [first_key(place) for place in range(NZ)]

    def first_pass(t, groups):
        rows_q = qg[pl.ds(4 * t, 4), 0].reshape(TILE, HD)
        rows_g = qg[pl.ds(4 * t, 4), 1].reshape(TILE, HD)
        rows_limit = jnp.concatenate([lim[2 * t], lim[2 * t + 1]], axis=1)
        for g in groups:
            low, high = GROUPS[g]
            count = (high - low) * KEYS
            keys = kv[0, low:high].reshape(count, HD)
            values = kv[1, low:high].reshape(count, HD)
            score = lax.dot_general(keys, rows_q, NT, preferred_element_type=F32) * SCORE
            index = lax.broadcasted_iota(jnp.int32, (KEYS, TILE), 0)
            masked = []
            for i, place in enumerate(range(low, high)):
                seen = index < rows_limit - starts[place]
                masked.append(jnp.where(seen, score[i * KEYS : (i + 1) * KEYS], NEG))
            score = jnp.concatenate(masked, axis=0)
            top = jnp.max(score, axis=0, keepdims=True)
            expon = jnp.exp2(score - top)
            product = lax.dot_general(values, rows_g, NT, preferred_element_type=F32)
            e_buf[t, low * KEYS : high * KEYS] = expon
            p_buf[t, low * KEYS : high * KEYS] = product
            mg[t, g : g + 1] = top
            tot[t, g : g + 1] = jnp.sum(expon, axis=0, keepdims=True)
            car[t, g : g + 1] = jnp.sum(expon * product, axis=0, keepdims=True)

    def run_first_pass(start, stop, groups):
        def step(t, carry):
            first_pass(t, groups)
            return carry

        lax.fori_loop(start, stop, step, 0)

    def close_rows(t, carry):
        highs = mg[t]
        top = jnp.max(highs, axis=0, keepdims=True)
        weight = jnp.exp2(highs - top)
        total = jnp.sum(tot[t] * weight, axis=0, keepdims=True)
        carried = jnp.sum(car[t] * weight, axis=0, keepdims=True)
        loc[t] = jnp.concatenate([top, carried / total], axis=0)
        stats = jnp.concatenate([top, total, carried, top], axis=0)
        stat_out[2 * t] = stats[:, : 2 * ROWS]
        stat_out[2 * t + 1] = stats[:, 2 * ROWS :]
        return carry

    def tile_wait(tiles):
        for t in tiles:
            for r in (2 * t, 2 * t + 1):
                if r:
                    rows_wait(2 * r + other)
                    arrived(lim.at[r], lim_send.at[1], lim_recv.at[r])

    plane_wait(1)
    kv_wait(0, 2)
    kv_to(0, 2, 4, up2)
    kv_to(0, 2, 3, up)
    kv_wait(0, 6)
    kv_to(0, 6, 5, down)
    kv_wait(1, 6)
    kv_to(1, 6, 4, down2)
    kv_to(1, 6, 5, down)
    kv_wait(1, 2)
    kv_to(1, 2, 3, up)
    plane_wait(2)
    for kind in range(2):
        for back in (1, 7):
            kv_wait(kind, back)
    tile_wait((0, 1))
    run_first_pass(0, 2, (0, 1))
    plane_wait(3)
    plane_wait(4)
    tile_wait((2, 3, 4))
    run_first_pass(2, 5, (0, 1))
    for kind in range(2):
        for back in (3, 5, 4):
            kv_wait(kind, back)
    run_first_pass(0, 5, (2,))
    tile_wait((5, 6, 7))
    run_first_pass(5, TILES, (0, 1, 2))
    lax.fori_loop(0, TILES, close_rows, 0)

    for r in farthest:
        for i, c in enumerate((core, other)):
            slot = 2 * SEEN[r] + core
            send(
                stat_out.at[r], stat_in.at[slot], st_send.at[2 * r + i], st_recv.at[slot],
                {**chips[r], "core": c},
            )
    send(stat_out.at[0], stat_in.at[core], st_send.at[0], st_recv.at[core], mate)
    stat_in[core] = stat_out[0]

    for place in range(NZ):
        kt[:, place * KEYS : (place + 1) * KEYS] = kv[0, place].astype(F32).T.astype(BF16)

    def query_products(t, carry):
        top, delta = loc[t, 0:1], loc[t, 1:2]
        expons, slopes = [], []
        for g, (low, high) in enumerate(GROUPS):
            weight = jnp.exp2(mg[t, g : g + 1] - top)
            expon = e_buf[t, low * KEYS : high * KEYS] * weight
            expons.append(expon.astype(BF16))
            slopes.append((expon * (p_buf[t, low * KEYS : high * KEYS] - delta)).astype(BF16))
        for i, right in enumerate((slopes, expons)):
            ab[t, i] = jnp.dot(kt[...], jnp.concatenate(right, axis=0), preferred_element_type=F32)
        return carry

    lax.fori_loop(0, TILES, query_products, 0)

    arrived(stat_in.at[other], st_send.at[0], st_recv.at[other])
    for r in nearest:
        for c in (core, other):
            arrived(stat_in.at[2 * r + c], st_send.at[0], st_recv.at[2 * r + c])
    top = own_high
    for i in range(PEERS):
        top = jnp.maximum(top, stat_in[i][0:1])
    weight = jnp.exp2(own_high - top)
    total, carried = own_total * weight, own_carry * weight
    for i in range(PEERS):
        stats = stat_in[i]
        weight = jnp.exp2(stats[0:1] - top)
        total += stats[1:2] * weight
        carried += stats[2:3] * weight
    inverse = 1.0 / total
    delta = carried * inverse
    final = jnp.concatenate([top, inverse, delta, top], axis=0)
    fin_out[...] = final
    fin[0] = final
    for r in farthest:
        send(fin_out, fin.at[SEEN[r]], fin_send.at[r], fin_recv.at[SEEN[r]], chips[r])

    self_probs = self_e[...] * (jnp.exp2(own_high - top) * inverse)
    self_slopes = (self_probs * (self_p[...] - delta)).astype(BF16)
    self_keys = ck_ref[...].astype(F32).T.astype(BF16)
    dq_self[...] = (jnp.dot(self_keys, self_slopes, preferred_element_type=F32) * SCALING).T

    for r in nearest:
        arrived(fin.at[r], fin_send.at[1], fin_recv.at[r])

    def close_weights(t, carry):
        final = jnp.concatenate([fin[2 * t], fin[2 * t + 1]], axis=1)
        mg[t] = jnp.exp2(mg[t] - final[0:1]) * final[1:2]
        return carry

    lax.fori_loop(0, TILES, close_weights, 0)

    def second_pass(place, carry):
        g = lax.div(place + 1, 3)
        grad_k = jnp.zeros((KEYS, HD), F32)
        grad_v = jnp.zeros((KEYS, HD), F32)
        for t in range(TILES):
            delta = jnp.concatenate([fin[2 * t, 2:3], fin[2 * t + 1, 2:3]], axis=1)
            at = pl.ds(pl.multiple_of(place * KEYS, KEYS), KEYS)
            probs = e_buf[t, at] * mg[t, pl.ds(g, 1)]
            slopes = (probs * (p_buf[t, at] - delta)).astype(BF16)
            rows_q = qg[4 * t : 4 * t + 4, 0].reshape(TILE, HD)
            rows_g = qg[4 * t : 4 * t + 4, 1].reshape(TILE, HD)
            grad_v += jnp.dot(probs.astype(BF16), rows_g, preferred_element_type=F32)
            grad_k += jnp.dot(slopes, rows_q, preferred_element_type=F32)
        part[place, 0] = grad_k * SCALING
        part[place, 1] = grad_v
        return carry

    def pass_on(kind, back, dst, sem, device, *more):
        at = PLACE[back]
        total = part[at, kind]
        for ref in more:
            total = total + ref[...].astype(F32)
        rs_out[kind, at] = total.astype(BF16)
        send(rs_out.at[kind, at], dst, rs_send.at[kind, at], sem, device)

    lax.fori_loop(0, 3, lambda i, c: second_pass(7 - i, c), 0)
    pass_on(0, 4, rs_far.at[0], far_recv.at[0], down2)
    pass_on(1, 4, rs_far.at[1], far_recv.at[1], up2)
    for kind in range(2):
        pass_on(kind, 3, rs_near.at[kind, 0], near_recv.at[kind, 0], down)
        pass_on(kind, 5, rs_near.at[kind, 1], near_recv.at[kind, 1], up)

    def query_pass(t, carry):
        final = jnp.concatenate([fin[2 * t], fin[2 * t + 1]], axis=1)
        weight = jnp.exp2(loc[t, 0:1] - final[0:1]) * final[1:2] * SCALING
        grads = (ab[t, 0] - ab[t, 1] * (final[2:3] - loc[t, 1:2])) * weight
        rows = grads.T.astype(BF16)
        for i in range(2):
            for c in range(2):
                at = (2 * i + c) * ROWS
                dq_out[c, 2 * t + i] = rows[at : at + ROWS]
        return carry

    lax.fori_loop(0, TILES, query_pass, 0)
    send(dq_out.at[other], dq_mate, mate_send, mate_recv, mate)
    lax.fori_loop(0, 3, lambda i, c: second_pass(4 - i, c), 0)
    arrived(dq_mate, mate_send, mate_recv)

    def add_mate(r, carry):
        dq_sum[r] = (dq_out[core, r].astype(F32) + dq_mate[r].astype(F32)).astype(BF16)
        return carry

    lax.fori_loop(0, CHIPS, add_mate, 0)
    for r in farthest:
        send(dq_sum.at[r], dq_in.at[SEEN[r]], dq_send.at[r], dq_recv.at[SEEN[r]], chips[r])
    lax.fori_loop(0, 2, lambda i, c: second_pass(1 - i, c), 0)
    for kind in range(2):
        pass_on(kind, 7, rs_end.at[kind, 2], end_recv.at[kind, 2], up)
        pass_on(kind, 1, rs_end.at[kind, 0], end_recv.at[kind, 0], down)

    def two_on(kind, way):
        arrived(rs_near.at[kind, way], rs_send.at[kind, 0], near_recv.at[kind, way])
        more = [rs_near.at[kind, way]]
        if kind == way:
            arrived(rs_far.at[way], rs_send.at[kind, 0], far_recv.at[way])
            more.append(rs_far.at[way])
        slot = 1 + 2 * way
        device = (down2, up2)[way]
        pass_on(
            kind, (2, 6)[way], rs_end.at[kind, slot], end_recv.at[kind, slot], device, *more
        )

    for kind, way in ((0, 0), (1, 1), (1, 0), (0, 1)):
        two_on(kind, way)

    grads = dq_self[pl.ds(pl.multiple_of(core * ROWS, ROWS), ROWS)] + dq_sum[0].astype(F32)
    for r in nearest:
        arrived(dq_in.at[r], dq_send.at[1], dq_recv.at[r])
        grads += dq_in[r].astype(F32)
    gq_ref[...] = jnp.concatenate(
        [grads[h * TOK : (h + 1) * TOK] for h in range(HEADS)], axis=1
    ).astype(BF16)
    for kind, out in enumerate((gk_ref, gv_ref)):
        total = part[0, kind]
        for way in (0, 2, 1, 3):
            arrived(rs_end.at[kind, way], rs_send.at[kind, 0], end_recv.at[kind, way])
            total = total + rs_end[kind, way].astype(F32)
        out[...] = total.astype(BF16)
    for copy in sent:
        copy.wait_send()


def body(queries, grad_out, prefix_keys, prefix_values, cand_keys, cand_values, lengths, offsets):
    vmem = pl.BlockSpec(memory_space=pltpu.VMEM)
    smem = pl.BlockSpec(memory_space=pltpu.SMEM)
    keys = NZ * KEYS
    block = cand_keys.shape[0]
    sem = pltpu.SemaphoreType.DMA
    return pl.pallas_call(
        kernel,
        out_shape=(
            jax.ShapeDtypeStruct(queries.shape, BF16),
            jax.ShapeDtypeStruct(prefix_keys.shape, BF16),
            jax.ShapeDtypeStruct(prefix_values.shape, BF16),
        ),
        in_specs=[vmem] * 6 + [smem] * 2,
        out_specs=(vmem,) * 3,
        scratch_shapes=[
            pltpu.VMEM((PEERS, 2, ROWS, HD), BF16),
            pltpu.VMEM((CHIPS, 1, 2 * ROWS), jnp.int32),
            pltpu.VMEM((2, NZ, KEYS, HD), BF16),
            pltpu.VMEM((HD, keys), BF16),
            pltpu.VMEM((TILES, keys, TILE), F32),
            pltpu.VMEM((TILES, keys, TILE), F32),
            pltpu.VMEM((TILES, len(GROUPS), TILE), F32),
            pltpu.VMEM((TILES, len(GROUPS), TILE), F32),
            pltpu.VMEM((TILES, len(GROUPS), TILE), F32),
            pltpu.VMEM((TILES, 2, TILE), F32),
            pltpu.VMEM((TILES, 2, HD, TILE), F32),
            pltpu.VMEM((CHIPS, 4, 2 * ROWS), F32),
            pltpu.VMEM((PEERS, 4, 2 * ROWS), F32),
            pltpu.VMEM((4, 2 * ROWS), F32),
            pltpu.VMEM((CHIPS, 4, 2 * ROWS), F32),
            pltpu.VMEM((block, 2 * ROWS), F32),
            pltpu.VMEM((block, 2 * ROWS), F32),
            pltpu.VMEM((2, CHIPS, ROWS, HD), BF16),
            pltpu.VMEM((CHIPS, ROWS, HD), BF16),
            pltpu.VMEM((CHIPS, ROWS, HD), BF16),
            pltpu.VMEM((CHIPS, ROWS, HD), BF16),
            pltpu.VMEM((2 * ROWS, HD), F32),
            pltpu.VMEM((NZ, 2, KEYS, HD), F32),
            pltpu.VMEM((2, NZ, KEYS, HD), BF16),
            pltpu.VMEM((2, 2, KEYS, HD), BF16),
            pltpu.VMEM((2, KEYS, HD), BF16),
            pltpu.VMEM((2, 4, KEYS, HD), BF16),
            sem((PEERS - 1,)),
            sem((PEERS,)),
            sem((CHIPS,)),
            sem((CHIPS,)),
            sem((2, NZ)),
            sem((2, NZ)),
            sem((PEERS,)),
            sem((PEERS,)),
            sem((CHIPS,)),
            sem((CHIPS,)),
            sem,
            sem,
            sem((CHIPS,)),
            sem((CHIPS,)),
            sem((2, NZ)),
            sem((2, 2)),
            sem((2,)),
            sem((2, 4)),
        ],
        compiler_params=pltpu.CompilerParams(
            collective_id=0, has_side_effects=True, vmem_limit_bytes=56 * 1024 * 1024
        ),
        name="attention_grads",
    )(queries, grad_out, prefix_keys, prefix_values, cand_keys, cand_values, lengths, offsets)


def solution(mesh):
    torus = Mesh(mesh.devices.reshape(NZ, 2, 2, NY, 2), AXES)
    in_specs = (
        P(CAND_CTX, None),
        P(CAND_CTX, None),
        P(CTX_CAND, None),
        P(CTX_CAND, None),
        P(CAND, None),
        P(CAND, None),
        P(CAND, None),
        P(CAND),
    )
    out_specs = (P(CAND_CTX, None), P(CTX_CAND, None), P(CTX_CAND, None))
    return jax.shard_map(body, mesh=torus, in_specs=in_specs, out_specs=out_specs, check_vma=False)
```

time: 65.4 us -> 55.9 us (0.85)
  Pallas kernels: 61.8 us -> 52.3 us
    pallas_call x1, Pallas kernels: 61.8 us -> 52.3 us  [body(): pl.pallas_call(kernel, out_shape=(jax.ShapeDtypeStruct(queries.shape, BF1...]
where the time goes in v2:
time: 55.9 us; the launch traced here: 55.6 us
  Pallas kernels  52.3 us (94%)
  local copies, waits for them, and re-layouts  2.72 us (5%)
  between operations  0.65 us (1%)
    pallas_call x1, Pallas kernels, body(): pl.pallas_call(kernel, out_shape=(jax.ShapeDtypeStruct(queries.shape, BF1...  52.3 us
    unnamed x7, local copies, waits for them, and re-layouts  2.72 us

profile of v2, /device:TPU:1, one launch (start us, length us, event | category | flops | bytes accessed | tf_op | source)
XLA Modules:
  0.0 55.6 jit_solution(10192135405705824781)
XLA Ops:
  0.6 52.3 %attention_grads.1 = (bf16[8,1024]{1,0:T(8,128)(2,1)}, bf16[128,128]{1,0:T(8,128)(2,1)}, bf16[128,128]{1,0:T(8,128)(2,1)}) custom-call(bf16[8,1024]{1,0:T(8,128)(2,1)} %q_ref.1, bf16[8,1024]{1,0:T(8,128)(2,1)} %g_ref.1, bf16[128,128]{1,0:T(8,128)(2,1)} %pk_ref.1, bf16[128,128]{1,0:T(8,128)(2,1)} %pv_ref.1, bf16[256,128]{1,0:T(8,128)(2,1)} %ck_ref.1, ...), custom_call_target="tpu_custom_call" | custom-call | tf_op jit(solution)/shard_map/attention_grads/pallas_call | solution.py:415
  52.9 0.0 copy-start.1
  52.9 1.3 %copy.14 = bf16[8,1024]{1,0:T(8,128)(2,1)} copy(bf16[8,1024]{1,0:T(8,128)(2,1)} %get-tuple-element.6) | data formatting | bytes 32768
  54.2 0.0 copy-done.1
  54.2 0.0 copy-start
  54.2 0.6 %copy.15 = bf16[128,128]{1,0:T(8,128)(2,1)} copy(bf16[128,128]{1,0:T(8,128)(2,1)S(1)} %copy-done.1) | data formatting | bytes 65536
  54.9 0.2 copy-done
  55.0 0.6 %copy.16 = bf16[128,128]{1,0:T(8,128)(2,1)} copy(bf16[128,128]{1,0:T(8,128)(2,1)S(1)} %copy-done) | data formatting | bytes 65536
Async XLA Ops:
  52.9 1.3 %copy-start.1 = (bf16[128,128]{1,0:T(8,128)(2,1)S(1)}, bf16[128,128]{1,0:T(8,128)(2,1)}, u32[]{:S(2)}) copy-start(bf16[128,128]{1,0:T(8,128)(2,1)} %get-tuple-element.7) | copy-start | bytes 98308
  54.2 0.8 %copy-start = (bf16[128,128]{1,0:T(8,128)(2,1)S(1)}, bf16[128,128]{1,0:T(8,128)(2,1)}, u32[]{:S(2)}) copy-start(bf16[128,128]{1,0:T(8,128)(2,1)} %get-tuple-element.8) | copy-start | bytes 98308

commit v3 on v2

--- a/solution.py
+++ b/solution.py
@@ -31,12 +31,14 @@
 SCORE = SCALING * math.log2(math.e)
 PLACE = {0: 0, 1: 1, 7: 2, 2: 3, 6: 4, 3: 5, 5: 6, 4: 7}
 BACK = {place: r for r, place in PLACE.items()}
-OFFSETS = sorted(
-    ((dx, dy) for dx in range(NX) for dy in range(NY)),
-    key=lambda o: min(o[0], NX - o[0]) + min(o[1], NY - o[1]),
-)
-FAR = [min(dx, NX - dx) + min(dy, NY - dy) for dx, dy in OFFSETS]
-SEEN = [OFFSETS.index(((NX - dx) % NX, (NY - dy) % NY)) for dx, dy in OFFSETS]
+STEPS = (0, 1, 3, 2)
+BACKWARD = (0, 2, 1, 3)
+HOPS = (0, 1, 1, 2)
+FAR = [HOPS[r // 4] + HOPS[r % 4] for r in range(CHIPS)]
+SEEN = [4 * BACKWARD[r // 4] + BACKWARD[r % 4] for r in range(CHIPS)]
+NEAREST = sorted(range(1, CHIPS), key=lambda r: FAR[r])
+FARTHEST = NEAREST[::-1]
+PIECE = 2 * ROWS + 16
 F32 = jnp.float32
 BF16 = jnp.bfloat16
 NT = (((1,), (1,)), ((), ()))
@@ -50,9 +52,9 @@
 def kernel(
     q_ref, g_ref, pk_ref, pv_ref, ck_ref, cv_ref, len_ref, off_ref,
     gq_ref, gk_ref, gv_ref,
-    qg, lim, kv, kt, e_buf, p_buf, mg, tot, car, loc, ab, stat_out, stat_in, fin_out, fin,
+    qg, kv, kt, e_buf, p_buf, mg, tot, car, loc, ab, stat_out, stat_in, fin_out, fin,
     self_e, self_p, dq_out, dq_mate, dq_sum, dq_in, dq_self, part, rs_out, rs_near, rs_far, rs_end,
-    qg_send, qg_recv, lim_send, lim_recv, kv_send, kv_recv,
+    qg_send, qg_recv, kv_send, kv_recv,
     st_send, st_recv, fin_send, fin_recv, mate_send, mate_recv, dq_send, dq_recv,
     rs_send, near_recv, far_recv, end_recv,
 ):
@@ -62,11 +64,18 @@
     mate = {"core": other}
     up, up2, down2, down = ({"z": lax.rem(z + d, NZ)} for d in (1, 2, NZ - 2, NZ - 1))
     chips = []
-    for dx, dy in OFFSETS:
-        px, py = lax.rem(x + dx, NX), lax.rem(y + dy, NY)
+    for r in range(CHIPS):
+        px, py = lax.rem(x + STEPS[r // 4], NX), lax.rem(y + STEPS[r % 4], NY)
         chips.append({"xh": lax.div(px, 2), "xl": lax.rem(px, 2), "y": py})
-    nearest = list(range(1, CHIPS))
-    farthest = nearest[::-1]
+
+    first_unit, second_unit = 1 + 3 * core, 4 - 3 * core
+
+    def along(axis, k):
+        px = lax.rem(x + STEPS[k] * (core if axis == 0 else other), NX)
+        py = lax.rem(y + STEPS[k] * (other if axis == 0 else core), NY)
+        return {"xh": lax.div(px, 2), "xl": lax.rem(px, 2), "y": py}
+
+    lines = [[along(axis, k) for k in range(4)] for axis in range(2)]
     sent = []
 
     def remote(src, dst, send_sem, recv_sem, device):
@@ -83,8 +92,8 @@
     def arrived(dst, send_sem, recv_sem):
         remote(dst, dst, send_sem, recv_sem, mate).wait_recv()
 
-    qg[core, 0] = stacked(q_ref[...]).astype(BF16)
-    qg[core, 1] = stacked(g_ref[...]).astype(BF16)
+    qg[core, 0:ROWS] = stacked(q_ref[...]).astype(BF16)
+    qg[core, ROWS : 2 * ROWS] = stacked(g_ref[...]).astype(BF16)
     kv[0, 0] = pk_ref[...]
     kv[1, 0] = pv_ref[...]
 
@@ -98,20 +107,19 @@
     lane = lax.broadcasted_iota(jnp.int32, (1, 2 * ROWS), 1)
     token = ((z * 2 + xh) * 2 + lax.div(lane, ROWS)) * TOK + lax.rem(lane, TOK)
     sample = sample_of(token)
-    limit = jnp.zeros_like(sample)
+    high, low = jnp.zeros((1, 2 * ROWS), F32), jnp.zeros((1, 2 * ROWS), F32)
     for s in range(SAMPLES):
-        limit = jnp.where(sample == s, off_ref[s], limit)
-    lim[0] = limit
+        mine = sample == s
+        high = jnp.where(mine, lax.div(off_ref[s], 256).astype(F32), high)
+        low = jnp.where(mine, lax.rem(off_ref[s], 256).astype(F32), low)
+    high, low = (jnp.broadcast_to(part_of, (8, 2 * ROWS)) for part_of in (high, low))
+    qg[core, 2 * ROWS : PIECE] = jnp.concatenate([high, low], axis=0).astype(BF16)
 
     barrier = pltpu.get_barrier_semaphore()
-    for r in nearest:
-        for c in (core, other):
-            pl.semaphore_signal(
-                barrier, inc=1, device_id={**chips[r], "core": c}, device_id_type=MESH
-            )
-    for device in (mate, up, down, up2, down2):
+    greeted = [mate, up, down, up2, down2] + lines[0][1:] + lines[1][1:]
+    for device in greeted:
         pl.semaphore_signal(barrier, inc=1, device_id=device, device_id_type=MESH)
-    pl.semaphore_wait(barrier, PEERS + 3)
+    pl.semaphore_wait(barrier, len(greeted))
 
     def kv_to(kind, back, new_back, device):
         src = (pk_ref, pv_ref)[kind] if back == 0 else kv.at[kind, PLACE[back]]
@@ -125,32 +133,39 @@
     def rows_wait(slot):
         arrived(qg.at[slot], qg_send.at[0], qg_recv.at[slot])
 
-    def hand_over(r):
-        slot = 2 * r + core
-        send(qg.at[slot], qg.at[slot], qg_send.at[r], qg_recv.at[slot], mate)
-
-    def plane_wait(far):
-        for r in nearest:
-            if FAR[r] == far:
-                rows_wait(2 * r + core)
-                hand_over(r)
+    def slot_of(first, second):
+        return 2 * (first * first_unit + second * second_unit) + core
+
+    rows_sent = iter(range(PEERS))
+
+    def rows_to(slot, there, device):
+        send(qg.at[slot], qg.at[there], qg_send.at[next(rows_sent)], qg_recv.at[there], device)
+
+    def second_line(first):
+        for k in (3, 1, 2):
+            rows_to(slot_of(first, 0), slot_of(first, BACKWARD[k]), lines[1][k])
+
+    def rows_from(first, second):
+        slot = slot_of(first, second)
+        rows_wait(slot)
+        if first and not second:
+            second_line(first)
+        rows_to(slot, slot, mate)
 
     for kind in range(2):
         kv_to(kind, 0, 2, up2)
         kv_to(kind, 0, 6, down2)
-    hand_over(0)
-    for r in farthest:
-        slot = 2 * SEEN[r] + core
-        send(qg.at[core], qg.at[slot], qg_send.at[CHIPS - 1 + r], qg_recv.at[slot], chips[r])
+    for k in (3, 1, 2):
+        rows_to(core, slot_of(BACKWARD[k], 0), lines[0][k])
+    rows_to(core, core, mate)
+    second_line(0)
     for kind in range(2):
         kv_to(kind, 0, 1, up)
         kv_to(kind, 0, 7, down)
-    for r in farthest:
-        send(lim.at[0], lim.at[SEEN[r]], lim_send.at[r], lim_recv.at[SEEN[r]], chips[r])
 
     rows_wait(other)
-    own_q = qg[0:2, 0].reshape(2 * ROWS, HD)
-    own_g = qg[0:2, 1].reshape(2 * ROWS, HD)
+    own_q = qg[0:2, 0:ROWS].reshape(2 * ROWS, HD)
+    own_g = qg[0:2, ROWS : 2 * ROWS].reshape(2 * ROWS, HD)
     block = ck_ref.shape[0]
     cand_token = lax.broadcasted_iota(jnp.int32, (block, 2 * ROWS), 0)
     allowed = (sample_of(cand_token) == sample) & (cand_token <= token)
@@ -168,19 +183,20 @@
         behind = lax.rem(z + NZ - BACK[place], NZ)
         return (((behind * 2 + xh) * 2 + core) * 8 + y * 2 + xl) * KEYS
 
-    starts = [first_key(place) for place in range(NZ)]
+    starts = [first_key(place).astype(F32) for place in range(NZ)]
 
     def first_pass(t, groups):
-        rows_q = qg[pl.ds(4 * t, 4), 0].reshape(TILE, HD)
-        rows_g = qg[pl.ds(4 * t, 4), 1].reshape(TILE, HD)
-        rows_limit = jnp.concatenate([lim[2 * t], lim[2 * t + 1]], axis=1)
+        rows_q = qg[pl.ds(4 * t, 4), 0:ROWS].reshape(TILE, HD)
+        rows_g = qg[pl.ds(4 * t, 4), ROWS : 2 * ROWS].reshape(TILE, HD)
+        coded = [qg[4 * t + 2 * i, 2 * ROWS : PIECE].astype(F32) for i in range(2)]
+        rows_limit = jnp.concatenate([c[0:1] * 256.0 + c[8:9] for c in coded], axis=1)
         for g in groups:
             low, high = GROUPS[g]
             count = (high - low) * KEYS
             keys = kv[0, low:high].reshape(count, HD)
             values = kv[1, low:high].reshape(count, HD)
             score = lax.dot_general(keys, rows_q, NT, preferred_element_type=F32) * SCORE
-            index = lax.broadcasted_iota(jnp.int32, (KEYS, TILE), 0)
+            index = lax.broadcasted_iota(jnp.int32, (KEYS, TILE), 0).astype(F32)
             masked = []
             for i, place in enumerate(range(low, high)):
                 seen = index < rows_limit - starts[place]
@@ -219,9 +235,9 @@
             for r in (2 * t, 2 * t + 1):
                 if r:
                     rows_wait(2 * r + other)
-                    arrived(lim.at[r], lim_send.at[1], lim_recv.at[r])
-
-    plane_wait(1)
+
+    for k in (1, 2, 3):
+        rows_from(k, 0)
     kv_wait(0, 2)
     kv_to(0, 2, 4, up2)
     kv_to(0, 2, 3, up)
@@ -232,25 +248,27 @@
     kv_to(1, 6, 5, down)
     kv_wait(1, 2)
     kv_to(1, 2, 3, up)
-    plane_wait(2)
+    for k in (1, 2, 3):
+        rows_from(0, k)
     for kind in range(2):
         for back in (1, 7):
             kv_wait(kind, back)
     tile_wait((0, 1))
     run_first_pass(0, 2, (0, 1))
-    plane_wait(3)
-    plane_wait(4)
-    tile_wait((2, 3, 4))
-    run_first_pass(2, 5, (0, 1))
+    for second in (1, 2, 3):
+        for first in (1, 2, 3):
+            rows_from(first, second)
+    tile_wait((2, 3, 4, 5))
+    run_first_pass(2, 6, (0, 1))
     for kind in range(2):
         for back in (3, 5, 4):
             kv_wait(kind, back)
-    run_first_pass(0, 5, (2,))
-    tile_wait((5, 6, 7))
-    run_first_pass(5, TILES, (0, 1, 2))
+    run_first_pass(0, 6, (2,))
+    tile_wait((6, 7))
+    run_first_pass(6, TILES, (0, 1, 2))
     lax.fori_loop(0, TILES, close_rows, 0)
 
-    for r in farthest:
+    for r in FARTHEST:
         for i, c in enumerate((core, other)):
             slot = 2 * SEEN[r] + core
             send(
@@ -278,7 +296,7 @@
     lax.fori_loop(0, TILES, query_products, 0)
 
     arrived(stat_in.at[other], st_send.at[0], st_recv.at[other])
-    for r in nearest:
+    for r in NEAREST:
         for c in (core, other):
             arrived(stat_in.at[2 * r + c], st_send.at[0], st_recv.at[2 * r + c])
     top = own_high
@@ -296,7 +314,7 @@
     final = jnp.concatenate([top, inverse, delta, top], axis=0)
     fin_out[...] = final
     fin[0] = final
-    for r in farthest:
+    for r in FARTHEST:
         send(fin_out, fin.at[SEEN[r]], fin_send.at[r], fin_recv.at[SEEN[r]], chips[r])
 
     self_probs = self_e[...] * (jnp.exp2(own_high - top) * inverse)
@@ -304,7 +322,7 @@
     self_keys = ck_ref[...].astype(F32).T.astype(BF16)
     dq_self[...] = (jnp.dot(self_keys, self_slopes, preferred_element_type=F32) * SCALING).T
 
-    for r in nearest:
+    for r in NEAREST:
         arrived(fin.at[r], fin_send.at[1], fin_recv.at[r])
 
     def close_weights(t, carry):
@@ -323,8 +341,8 @@
             at = pl.ds(pl.multiple_of(place * KEYS, KEYS), KEYS)
             probs = e_buf[t, at] * mg[t, pl.ds(g, 1)]
             slopes = (probs * (p_buf[t, at] - delta)).astype(BF16)
-            rows_q = qg[4 * t : 4 * t + 4, 0].reshape(TILE, HD)
-            rows_g = qg[4 * t : 4 * t + 4, 1].reshape(TILE, HD)
+            rows_q = qg[4 * t : 4 * t + 4, 0:ROWS].reshape(TILE, HD)
+            rows_g = qg[4 * t : 4 * t + 4, ROWS : 2 * ROWS].reshape(TILE, HD)
             grad_v += jnp.dot(probs.astype(BF16), rows_g, preferred_element_type=F32)
             grad_k += jnp.dot(slopes, rows_q, preferred_element_type=F32)
         part[place, 0] = grad_k * SCALING
@@ -367,7 +385,7 @@
         return carry
 
     lax.fori_loop(0, CHIPS, add_mate, 0)
-    for r in farthest:
+    for r in FARTHEST:
         send(dq_sum.at[r], dq_in.at[SEEN[r]], dq_send.at[r], dq_recv.at[SEEN[r]], chips[r])
     lax.fori_loop(0, 2, lambda i, c: second_pass(1 - i, c), 0)
     for kind in range(2):
@@ -390,7 +408,7 @@
         two_on(kind, way)
 
     grads = dq_self[pl.ds(pl.multiple_of(core * ROWS, ROWS), ROWS)] + dq_sum[0].astype(F32)
-    for r in nearest:
+    for r in NEAREST:
         arrived(dq_in.at[r], dq_send.at[1], dq_recv.at[r])
         grads += dq_in[r].astype(F32)
     gq_ref[...] = jnp.concatenate(
@@ -422,8 +440,7 @@
         in_specs=[vmem] * 6 + [smem] * 2,
         out_specs=(vmem,) * 3,
         scratch_shapes=[
-            pltpu.VMEM((PEERS, 2, ROWS, HD), BF16),
-            pltpu.VMEM((CHIPS, 1, 2 * ROWS), jnp.int32),
+            pltpu.VMEM((PEERS, PIECE, HD), BF16),
             pltpu.VMEM((2, NZ, KEYS, HD), BF16),
             pltpu.VMEM((HD, keys), BF16),
             pltpu.VMEM((TILES, keys, TILE), F32),
@@ -449,10 +466,8 @@
             pltpu.VMEM((2, 2, KEYS, HD), BF16),
             pltpu.VMEM((2, KEYS, HD), BF16),
             pltpu.VMEM((2, 4, KEYS, HD), BF16),
-            sem((PEERS - 1,)),
             sem((PEERS,)),
-            sem((CHIPS,)),
-            sem((CHIPS,)),
+            sem((PEERS,)),
             sem((2, NZ)),
             sem((2, NZ)),
             sem((PEERS,)),

time: 55.9 us -> 52.8 us (0.945)
  Pallas kernels: 52.3 us -> 49.1 us
    pallas_call x1, Pallas kernels: 52.3 us -> 49.1 us  [body(): pl.pallas_call(kernel, out_shape=(jax.ShapeDtypeStruct(queries.shape, BF1...]
where the time goes in v3:
time: 52.8 us; the launch traced here: 52.5 us
  Pallas kernels  49.1 us (93%)
  local copies, waits for them, and re-layouts  2.72 us (5%)
  between operations  0.65 us (1%)
    pallas_call x1, Pallas kernels, body(): pl.pallas_call(kernel, out_shape=(jax.ShapeDtypeStruct(queries.shape, BF1...  49.1 us
    unnamed x7, local copies, waits for them, and re-layouts  2.72 us

profile of v3, /device:TPU:1, one launch (start us, length us, event | category | flops | bytes accessed | tf_op | source)
XLA Modules:
  0.0 52.5 jit_solution(4855021178328452426)
XLA Ops:
  0.6 49.1 %attention_grads.1 = (bf16[8,1024]{1,0:T(8,128)(2,1)}, bf16[128,128]{1,0:T(8,128)(2,1)}, bf16[128,128]{1,0:T(8,128)(2,1)}) custom-call(bf16[8,1024]{1,0:T(8,128)(2,1)} %q_ref.1, bf16[8,1024]{1,0:T(8,128)(2,1)} %g_ref.1, bf16[128,128]{1,0:T(8,128)(2,1)} %pk_ref.1, bf16[128,128]{1,0:T(8,128)(2,1)} %pv_ref.1, bf16[256,128]{1,0:T(8,128)(2,1)} %ck_ref.1, ...), custom_call_target="tpu_custom_call" | custom-call | tf_op jit(solution)/shard_map/attention_grads/pallas_call | solution.py:433
  49.8 0.0 copy-start.1
  49.8 1.3 %copy.14 = bf16[8,1024]{1,0:T(8,128)(2,1)} copy(bf16[8,1024]{1,0:T(8,128)(2,1)} %get-tuple-element.6) | data formatting | bytes 32768
  51.1 0.0 copy-done.1
  51.1 0.0 copy-start
  51.1 0.6 %copy.15 = bf16[128,128]{1,0:T(8,128)(2,1)} copy(bf16[128,128]{1,0:T(8,128)(2,1)S(1)} %copy-done.1) | data formatting | bytes 65536
  51.7 0.2 copy-done
  51.9 0.6 %copy.16 = bf16[128,128]{1,0:T(8,128)(2,1)} copy(bf16[128,128]{1,0:T(8,128)(2,1)S(1)} %copy-done) | data formatting | bytes 65536
Async XLA Ops:
  49.8 1.3 %copy-start.1 = (bf16[128,128]{1,0:T(8,128)(2,1)S(1)}, bf16[128,128]{1,0:T(8,128)(2,1)}, u32[]{:S(2)}) copy-start(bf16[128,128]{1,0:T(8,128)(2,1)} %get-tuple-element.7) | copy-start | bytes 98308
  51.1 0.8 %copy-start = (bf16[128,128]{1,0:T(8,128)(2,1)S(1)}, bf16[128,128]{1,0:T(8,128)(2,1)}, u32[]{:S(2)}) copy-start(bf16[128,128]{1,0:T(8,128)(2,1)} %get-tuple-element.8) | copy-start | bytes 98308

commit v4 on v3

--- a/solution.py
+++ b/solution.py
@@ -34,8 +34,12 @@
 STEPS = (0, 1, 3, 2)
 BACKWARD = (0, 2, 1, 3)
 HOPS = (0, 1, 1, 2)
-FAR = [HOPS[r // 4] + HOPS[r % 4] for r in range(CHIPS)]
-SEEN = [4 * BACKWARD[r // 4] + BACKWARD[r % 4] for r in range(CHIPS)]
+ORDER = (
+    (0, 0), (0, 1), (1, 0), (0, 2), (2, 0), (0, 3), (3, 0), (1, 1),
+    (2, 1), (1, 2), (2, 2), (1, 3), (3, 1), (2, 3), (3, 2), (3, 3),
+)
+FAR = [HOPS[a] + HOPS[b] for a, b in ORDER]
+SEEN = [ORDER.index((BACKWARD[a], BACKWARD[b])) for a, b in ORDER]
 NEAREST = sorted(range(1, CHIPS), key=lambda r: FAR[r])
 FARTHEST = NEAREST[::-1]
 PIECE = 2 * ROWS + 16
@@ -50,9 +54,9 @@
 
 
 def kernel(
-    q_ref, g_ref, pk_ref, pv_ref, ck_ref, cv_ref, len_ref, off_ref,
+    q_hbm, g_hbm, pk_hbm, pv_hbm, ck_hbm, cv_hbm, len_hbm, off_hbm,
     gq_ref, gk_ref, gv_ref,
-    qg, kv, kt, e_buf, p_buf, mg, tot, car, loc, ab, stat_out, stat_in, fin_out, fin,
+    q_ref, g_ref, ck_ref, cv_ref, len_ref, off_ref, in_sem, qg, kv, kt, e_buf, p_buf, mg, tot, car, loc, ab, stat_out, stat_in, fin_out, fin,
     self_e, self_p, dq_out, dq_mate, dq_sum, dq_in, dq_self, part, rs_out, rs_near, rs_far, rs_end,
     qg_send, qg_recv, kv_send, kv_recv,
     st_send, st_recv, fin_send, fin_recv, mate_send, mate_recv, dq_send, dq_recv,
@@ -65,10 +69,8 @@
     up, up2, down2, down = ({"z": lax.rem(z + d, NZ)} for d in (1, 2, NZ - 2, NZ - 1))
     chips = []
     for r in range(CHIPS):
-        px, py = lax.rem(x + STEPS[r // 4], NX), lax.rem(y + STEPS[r % 4], NY)
+        px, py = lax.rem(x + STEPS[ORDER[r][0]], NX), lax.rem(y + STEPS[ORDER[r][1]], NY)
         chips.append({"xh": lax.div(px, 2), "xl": lax.rem(px, 2), "y": py})
-
-    first_unit, second_unit = 1 + 3 * core, 4 - 3 * core
 
     def along(axis, k):
         px = lax.rem(x + STEPS[k] * (core if axis == 0 else other), NX)
@@ -92,10 +94,26 @@
     def arrived(dst, send_sem, recv_sem):
         remote(dst, dst, send_sem, recv_sem, mate).wait_recv()
 
+    inputs = [
+        pltpu.make_async_copy(src, dst, in_sem.at[i])
+        for i, (src, dst) in enumerate(
+            (
+                (pk_hbm, kv.at[0, 0]), (pv_hbm, kv.at[1, 0]), (q_hbm, q_ref), (g_hbm, g_ref),
+                (len_hbm, len_ref), (off_hbm, off_ref), (ck_hbm, ck_ref), (cv_hbm, cv_ref),
+            )
+        )
+    ]
+    for copy in inputs:
+        copy.start()
+    barrier = pltpu.get_barrier_semaphore()
+    greeted = [mate, up, down, up2, down2] + lines[0][1:] + lines[1][1:]
+    for device in greeted:
+        pl.semaphore_signal(barrier, inc=1, device_id=device, device_id_type=MESH)
+    for copy in inputs[2:6]:
+        copy.wait()
+
     qg[core, 0:ROWS] = stacked(q_ref[...]).astype(BF16)
     qg[core, ROWS : 2 * ROWS] = stacked(g_ref[...]).astype(BF16)
-    kv[0, 0] = pk_ref[...]
-    kv[1, 0] = pv_ref[...]
 
     ends = [len_ref[0, 0]]
     for s in range(1, SAMPLES):
@@ -115,16 +133,13 @@
     high, low = (jnp.broadcast_to(part_of, (8, 2 * ROWS)) for part_of in (high, low))
     qg[core, 2 * ROWS : PIECE] = jnp.concatenate([high, low], axis=0).astype(BF16)
 
-    barrier = pltpu.get_barrier_semaphore()
-    greeted = [mate, up, down, up2, down2] + lines[0][1:] + lines[1][1:]
-    for device in greeted:
-        pl.semaphore_signal(barrier, inc=1, device_id=device, device_id_type=MESH)
+    for copy in inputs[:2]:
+        copy.wait()
     pl.semaphore_wait(barrier, len(greeted))
 
     def kv_to(kind, back, new_back, device):
-        src = (pk_ref, pv_ref)[kind] if back == 0 else kv.at[kind, PLACE[back]]
         at = PLACE[new_back]
-        send(src, kv.at[kind, at], kv_send.at[kind, at], kv_recv.at[kind, at], device)
+        send(kv.at[kind, PLACE[back]], kv.at[kind, at], kv_send.at[kind, at], kv_recv.at[kind, at], device)
 
     def kv_wait(kind, back):
         at = PLACE[back]
@@ -134,7 +149,7 @@
         arrived(qg.at[slot], qg_send.at[0], qg_recv.at[slot])
 
     def slot_of(first, second):
-        return 2 * (first * first_unit + second * second_unit) + core
+        return 2 * (other * ORDER.index((second, first)) + core * ORDER.index((first, second))) + core
 
     rows_sent = iter(range(PEERS))
 
@@ -163,6 +178,8 @@
         kv_to(kind, 0, 1, up)
         kv_to(kind, 0, 7, down)
 
+    for copy in inputs[6:]:
+        copy.wait()
     rows_wait(other)
     own_q = qg[0:2, 0:ROWS].reshape(2 * ROWS, HD)
     own_g = qg[0:2, ROWS : 2 * ROWS].reshape(2 * ROWS, HD)
@@ -233,7 +250,7 @@
     def tile_wait(tiles):
         for t in tiles:
             for r in (2 * t, 2 * t + 1):
-                if r:
+                if not (isinstance(r, int) and r == 0):
                     rows_wait(2 * r + other)
 
     for k in (1, 2, 3):
@@ -253,19 +270,23 @@
     for kind in range(2):
         for back in (1, 7):
             kv_wait(kind, back)
-    tile_wait((0, 1))
-    run_first_pass(0, 2, (0, 1))
-    for second in (1, 2, 3):
-        for first in (1, 2, 3):
-            rows_from(first, second)
-    tile_wait((2, 3, 4, 5))
-    run_first_pass(2, 6, (0, 1))
+    tile_wait((0, 1, 2))
+    run_first_pass(0, 3, (0, 1))
+    for first, second in ((1, 1), (2, 1), (1, 2), (2, 2)):
+        rows_from(first, second)
     for kind in range(2):
         for back in (3, 5, 4):
             kv_wait(kind, back)
-    run_first_pass(0, 6, (2,))
-    tile_wait((6, 7))
-    run_first_pass(6, TILES, (0, 1, 2))
+    run_first_pass(0, 3, (2,))
+    for first, second in ((3, 1), (3, 2), (1, 3), (2, 3), (3, 3)):
+        rows_from(first, second)
+
+    def last_tiles(t, carry):
+        tile_wait((t,))
+        first_pass(t, (0, 1, 2))
+        return carry
+
+    lax.fori_loop(3, TILES, last_tiles, 0)
     lax.fori_loop(0, TILES, close_rows, 0)
 
     for r in FARTHEST:
@@ -357,11 +378,14 @@
         rs_out[kind, at] = total.astype(BF16)
         send(rs_out.at[kind, at], dst, rs_send.at[kind, at], sem, device)
 
-    lax.fori_loop(0, 3, lambda i, c: second_pass(7 - i, c), 0)
+    second_pass(PLACE[4], 0)
     pass_on(0, 4, rs_far.at[0], far_recv.at[0], down2)
     pass_on(1, 4, rs_far.at[1], far_recv.at[1], up2)
+    second_pass(PLACE[3], 0)
     for kind in range(2):
         pass_on(kind, 3, rs_near.at[kind, 0], near_recv.at[kind, 0], down)
+    second_pass(PLACE[5], 0)
+    for kind in range(2):
         pass_on(kind, 5, rs_near.at[kind, 1], near_recv.at[kind, 1], up)
 
     def query_pass(t, carry):
@@ -377,7 +401,10 @@
 
     lax.fori_loop(0, TILES, query_pass, 0)
     send(dq_out.at[other], dq_mate, mate_send, mate_recv, mate)
-    lax.fori_loop(0, 3, lambda i, c: second_pass(4 - i, c), 0)
+    lax.fori_loop(0, 2, lambda i, c: second_pass(2 - i, c), 0)
+    for kind in range(2):
+        pass_on(kind, 7, rs_end.at[kind, 2], end_recv.at[kind, 2], up)
+        pass_on(kind, 1, rs_end.at[kind, 0], end_recv.at[kind, 0], down)
     arrived(dq_mate, mate_send, mate_recv)
 
     def add_mate(r, carry):
@@ -387,10 +414,7 @@
     lax.fori_loop(0, CHIPS, add_mate, 0)
     for r in FARTHEST:
         send(dq_sum.at[r], dq_in.at[SEEN[r]], dq_send.at[r], dq_recv.at[SEEN[r]], chips[r])
-    lax.fori_loop(0, 2, lambda i, c: second_pass(1 - i, c), 0)
-    for kind in range(2):
-        pass_on(kind, 7, rs_end.at[kind, 2], end_recv.at[kind, 2], up)
-        pass_on(kind, 1, rs_end.at[kind, 0], end_recv.at[kind, 0], down)
+    lax.fori_loop(0, 2, lambda i, c: second_pass(4 - i, c), 0)
 
     def two_on(kind, way):
         arrived(rs_near.at[kind, way], rs_send.at[kind, 0], near_recv.at[kind, way])
@@ -404,8 +428,9 @@
             kind, (2, 6)[way], rs_end.at[kind, slot], end_recv.at[kind, slot], device, *more
         )
 
-    for kind, way in ((0, 0), (1, 1), (1, 0), (0, 1)):
+    for kind, way in ((1, 0), (0, 1), (0, 0), (1, 1)):
         two_on(kind, way)
+    second_pass(0, 0)
 
     grads = dq_self[pl.ds(pl.multiple_of(core * ROWS, ROWS), ROWS)] + dq_sum[0].astype(F32)
     for r in NEAREST:
@@ -424,22 +449,38 @@
         copy.wait_send()
 
 
+def store(*refs):
+    sems = refs[6]
+    copies = [pltpu.make_async_copy(refs[i], refs[3 + i], sems.at[i]) for i in range(3)]
+    for copy in copies:
+        copy.start()
+    for copy in copies:
+        copy.wait()
+
+
 def body(queries, grad_out, prefix_keys, prefix_values, cand_keys, cand_values, lengths, offsets):
     vmem = pl.BlockSpec(memory_space=pltpu.VMEM)
-    smem = pl.BlockSpec(memory_space=pltpu.SMEM)
+    anywhere = pl.BlockSpec(memory_space=pl.ANY)
     keys = NZ * KEYS
     block = cand_keys.shape[0]
     sem = pltpu.SemaphoreType.DMA
-    return pl.pallas_call(
+    found = pl.pallas_call(
         kernel,
         out_shape=(
-            jax.ShapeDtypeStruct(queries.shape, BF16),
-            jax.ShapeDtypeStruct(prefix_keys.shape, BF16),
-            jax.ShapeDtypeStruct(prefix_values.shape, BF16),
+            pltpu.VMEM(queries.shape, BF16),
+            pltpu.VMEM(prefix_keys.shape, BF16),
+            pltpu.VMEM(prefix_values.shape, BF16),
         ),
-        in_specs=[vmem] * 6 + [smem] * 2,
+        in_specs=[anywhere] * 8,
         out_specs=(vmem,) * 3,
         scratch_shapes=[
+            pltpu.VMEM(queries.shape, BF16),
+            pltpu.VMEM(grad_out.shape, BF16),
+            pltpu.VMEM(cand_keys.shape, BF16),
+            pltpu.VMEM(cand_values.shape, BF16),
+            pltpu.SMEM(lengths.shape, jnp.int32),
+            pltpu.SMEM(offsets.shape, jnp.int32),
+            sem((8,)),
             pltpu.VMEM((PEERS, PIECE, HD), BF16),
             pltpu.VMEM((2, NZ, KEYS, HD), BF16),
             pltpu.VMEM((HD, keys), BF16),
@@ -488,6 +529,14 @@
         ),
         name="attention_grads",
     )(queries, grad_out, prefix_keys, prefix_values, cand_keys, cand_values, lengths, offsets)
+    return pl.pallas_call(
+        store,
+        out_shape=tuple(jax.ShapeDtypeStruct(a.shape, BF16) for a in found),
+        in_specs=[vmem] * 3,
+        out_specs=(anywhere,) * 3,
+        scratch_shapes=[sem((3,))],
+        name="store",
+    )(*(pltpu.with_memory_space_constraint(a, pltpu.VMEM) for a in found))
 
 
 def solution(mesh):

time: 52.8 us -> 46.6 us (0.88)
  Pallas kernels: 49.1 us -> 45.8 us
  local copies, waits for them, and re-layouts: 2.72 us -> 0 us
    pallas_call x1 -> x2, Pallas kernels: 49.1 us -> 45.8 us  [the longest x1 45.2 us: body(): pl.pallas_call(kernel, out_shape=(pltpu.VMEM(queries.shape, BF16), pltpu....]
    unnamed x7 -> x0, local copies, waits for them, and re-layouts: 2.72 us -> none
where the time goes in v4:
time: 46.6 us; the launch traced here: 46.5 us
  Pallas kernels  45.8 us (98%)
  between operations  0.64 us (1%)
    pallas_call x1, Pallas kernels, body(): pl.pallas_call(kernel, out_shape=(pltpu.VMEM(queries.shape, BF16), pltpu....  45.2 us

profile of v4, /device:TPU:1, one launch (start us, length us, event | category | flops | bytes accessed | tf_op | source)
XLA Modules:
  0.0 46.5 jit_solution(5501988085705778727)
XLA Ops:
  0.6 45.2 %attention_grads.1 = (bf16[8,1024]{1,0:T(8,128)(2,1)S(1)}, bf16[128,128]{1,0:T(8,128)(2,1)S(1)}, bf16[128,128]{1,0:T(8,128)(2,1)S(1)}) custom-call(bf16[8,1024]{1,0:T(8,128)(2,1)} %q_hbm.1, bf16[8,1024]{1,0:T(8,128)(2,1)} %g_hbm.1, bf16[128,128]{1,0:T(8,128)(2,1)} %pk_hbm.1, bf16[128,128]{1,0:T(8,128)(2,1)} %pv_hbm.1, bf16[256,128]{1,0:T(8,128)(2,1)} %ck_hbm.1, ...), custom_call_target="tpu_custom_call" | custom-call | tf_op jit(solution)/shard_map/attention_grads/pallas_call | solution.py:467
  45.8 0.7 %store.1 = (bf16[8,1024]{1,0:T(8,128)(2,1)}, bf16[128,128]{1,0:T(8,128)(2,1)}, bf16[128,128]{1,0:T(8,128)(2,1)}) custom-call(bf16[8,1024]{1,0:T(8,128)(2,1)S(1)} %get-tuple-element.6.refs_0_, bf16[128,128]{1,0:T(8,128)(2,1)S(1)} %get-tuple-element.7.refs_1_, bf16[128,128]{1,0:T(8,128)(2,1)S(1)} %get-tuple-element.8.refs_2_), custom_call_target="tpu_custom_call" | custom-call | tf_op jit(solution)/shard_map/store/pallas_call | solution.py:532

commit v5 on v4

--- a/solution.py
+++ b/solution.py
@@ -56,10 +56,10 @@
 def kernel(
     q_hbm, g_hbm, pk_hbm, pv_hbm, ck_hbm, cv_hbm, len_hbm, off_hbm,
     gq_ref, gk_ref, gv_ref,
-    q_ref, g_ref, ck_ref, cv_ref, len_ref, off_ref, in_sem, qg, kv, kt, e_buf, p_buf, mg, tot, car, loc, ab, stat_out, stat_in, fin_out, fin,
-    self_e, self_p, dq_out, dq_mate, dq_sum, dq_in, dq_self, part, rs_out, rs_near, rs_far, rs_end,
+    q_ref, g_ref, ck_ref, cv_ref, len_ref, off_ref, in_sem, qg, kv, kt, e_buf, p_buf, mg, tot, car, loc, ab, ab_mate, stat_out, stat_in, stat_mate, fin_out, fin,
+    self_e, self_p, dq_out, dq_in, dq_self, part, rs_out, rs_near, rs_far, rs_end,
     qg_send, qg_recv, kv_send, kv_recv,
-    st_send, st_recv, fin_send, fin_recv, mate_send, mate_recv, dq_send, dq_recv,
+    st_send, st_recv, fin_send, fin_recv, mate_send, mate_recv, ab_send, ab_recv, dq_send, dq_recv,
     rs_send, near_recv, far_recv, end_recv,
 ):
     z, xh, core, y, xl = (lax.axis_index(a) for a in AXES)
@@ -241,7 +241,6 @@
         weight = jnp.exp2(highs - top)
         total = jnp.sum(tot[t] * weight, axis=0, keepdims=True)
         carried = jnp.sum(car[t] * weight, axis=0, keepdims=True)
-        loc[t] = jnp.concatenate([top, carried / total], axis=0)
         stats = jnp.concatenate([top, total, carried, top], axis=0)
         stat_out[2 * t] = stats[:, : 2 * ROWS]
         stat_out[2 * t + 1] = stats[:, 2 * ROWS :]
@@ -289,21 +288,27 @@
     lax.fori_loop(3, TILES, last_tiles, 0)
     lax.fori_loop(0, TILES, close_rows, 0)
 
+    send(stat_out, stat_mate, mate_send, mate_recv, mate)
     for r in FARTHEST:
-        for i, c in enumerate((core, other)):
-            slot = 2 * SEEN[r] + core
-            send(
-                stat_out.at[r], stat_in.at[slot], st_send.at[2 * r + i], st_recv.at[slot],
-                {**chips[r], "core": c},
-            )
-    send(stat_out.at[0], stat_in.at[core], st_send.at[0], st_recv.at[core], mate)
-    stat_in[core] = stat_out[0]
+        slot = 2 * SEEN[r] + core
+        send(
+            stat_out.at[r], stat_in.at[slot], st_send.at[r], st_recv.at[slot],
+            {**chips[r], "core": 1},
+        )
 
     for place in range(NZ):
         kt[:, place * KEYS : (place + 1) * KEYS] = kv[0, place].astype(F32).T.astype(BF16)
 
+    arrived(stat_mate, mate_send, mate_recv)
+
     def query_products(t, carry):
-        top, delta = loc[t, 0:1], loc[t, 1:2]
+        pair = [
+            jnp.concatenate([ref[2 * t], ref[2 * t + 1]], axis=1) for ref in (stat_out, stat_mate)
+        ]
+        top = jnp.maximum(pair[0][0:1], pair[1][0:1])
+        scaled = [part_of * jnp.exp2(part_of[0:1] - top) for part_of in pair]
+        delta = (scaled[0][2:3] + scaled[1][2:3]) / (scaled[0][1:2] + scaled[1][1:2])
+        loc[t] = jnp.concatenate([top, delta], axis=0)
         expons, slopes = [], []
         for g, (low, high) in enumerate(GROUPS):
             weight = jnp.exp2(mg[t, g : g + 1] - top)
@@ -312,37 +317,54 @@
             slopes.append((expon * (p_buf[t, low * KEYS : high * KEYS] - delta)).astype(BF16))
         for i, right in enumerate((slopes, expons)):
             ab[t, i] = jnp.dot(kt[...], jnp.concatenate(right, axis=0), preferred_element_type=F32)
+        remote(ab.at[t], ab_mate.at[t], ab_send.at[t], ab_recv.at[t], mate).start()
         return carry
 
     lax.fori_loop(0, TILES, query_products, 0)
 
-    arrived(stat_in.at[other], st_send.at[0], st_recv.at[other])
-    for r in NEAREST:
-        for c in (core, other):
-            arrived(stat_in.at[2 * r + c], st_send.at[0], st_recv.at[2 * r + c])
-    top = own_high
-    for i in range(PEERS):
-        top = jnp.maximum(top, stat_in[i][0:1])
-    weight = jnp.exp2(own_high - top)
-    total, carried = own_total * weight, own_carry * weight
-    for i in range(PEERS):
-        stats = stat_in[i]
-        weight = jnp.exp2(stats[0:1] - top)
-        total += stats[1:2] * weight
-        carried += stats[2:3] * weight
-    inverse = 1.0 / total
-    delta = carried * inverse
-    final = jnp.concatenate([top, inverse, delta, top], axis=0)
-    fin_out[...] = final
-    fin[0] = final
-    for r in FARTHEST:
-        send(fin_out, fin.at[SEEN[r]], fin_send.at[r], fin_recv.at[SEEN[r]], chips[r])
-
-    self_probs = self_e[...] * (jnp.exp2(own_high - top) * inverse)
-    self_slopes = (self_probs * (self_p[...] - delta)).astype(BF16)
-    self_keys = ck_ref[...].astype(F32).T.astype(BF16)
-    dq_self[...] = (jnp.dot(self_keys, self_slopes, preferred_element_type=F32) * SCALING).T
-
+    def final_sends():
+        copies = []
+        for r in FARTHEST:
+            for c in (0, 1):
+                copies.append(
+                    remote(
+                        fin_out, fin.at[SEEN[r]], fin_send.at[2 * r + c], fin_recv.at[SEEN[r]],
+                        {**chips[r], "core": c},
+                    )
+                )
+        copies.append(remote(fin_out, fin.at[0], fin_send.at[0], fin_recv.at[0], {"core": 0}))
+        return copies
+
+    @pl.when(core == 1)
+    def _():
+        for r in NEAREST:
+            for c in range(2):
+                arrived(stat_in.at[2 * r + c], st_send.at[1], st_recv.at[2 * r + c])
+        stat_in[0] = stat_mate[0]
+        stat_in[1] = stat_out[0]
+        top = own_high
+        for i in range(PEERS):
+            top = jnp.maximum(top, stat_in[i][0:1])
+        weight = jnp.exp2(own_high - top)
+        total, carried = own_total * weight, own_carry * weight
+        for i in range(PEERS):
+            stats = stat_in[i]
+            weight = jnp.exp2(stats[0:1] - top)
+            total += stats[1:2] * weight
+            carried += stats[2:3] * weight
+        inverse = 1.0 / total
+        final = jnp.concatenate([top, inverse, carried * inverse, top], axis=0)
+        fin_out[...] = final
+        fin[0] = final
+        for copy in final_sends():
+            copy.start()
+
+    @pl.when(core == 0)
+    def _():
+        arrived(fin.at[0], fin_send.at[0], fin_recv.at[0])
+
+    for t in range(TILES):
+        remote(ab.at[t], ab_mate.at[t], ab_send.at[t], ab_recv.at[t], mate).wait()
     for r in NEAREST:
         arrived(fin.at[r], fin_send.at[1], fin_recv.at[r])
 
@@ -391,7 +413,8 @@
     def query_pass(t, carry):
         final = jnp.concatenate([fin[2 * t], fin[2 * t + 1]], axis=1)
         weight = jnp.exp2(loc[t, 0:1] - final[0:1]) * final[1:2] * SCALING
-        grads = (ab[t, 0] - ab[t, 1] * (final[2:3] - loc[t, 1:2])) * weight
+        slopes, expons = (ab[t, i] + ab_mate[t, i] for i in range(2))
+        grads = (slopes - expons * (final[2:3] - loc[t, 1:2])) * weight
         rows = grads.T.astype(BF16)
         for i in range(2):
             for c in range(2):
@@ -400,20 +423,12 @@
         return carry
 
     lax.fori_loop(0, TILES, query_pass, 0)
-    send(dq_out.at[other], dq_mate, mate_send, mate_recv, mate)
+    for r in FARTHEST:
+        send(dq_out.at[core, r], dq_in.at[SEEN[r]], dq_send.at[r], dq_recv.at[SEEN[r]], chips[r])
     lax.fori_loop(0, 2, lambda i, c: second_pass(2 - i, c), 0)
     for kind in range(2):
         pass_on(kind, 7, rs_end.at[kind, 2], end_recv.at[kind, 2], up)
         pass_on(kind, 1, rs_end.at[kind, 0], end_recv.at[kind, 0], down)
-    arrived(dq_mate, mate_send, mate_recv)
-
-    def add_mate(r, carry):
-        dq_sum[r] = (dq_out[core, r].astype(F32) + dq_mate[r].astype(F32)).astype(BF16)
-        return carry
-
-    lax.fori_loop(0, CHIPS, add_mate, 0)
-    for r in FARTHEST:
-        send(dq_sum.at[r], dq_in.at[SEEN[r]], dq_send.at[r], dq_recv.at[SEEN[r]], chips[r])
     lax.fori_loop(0, 2, lambda i, c: second_pass(4 - i, c), 0)
 
     def two_on(kind, way):
@@ -428,11 +443,16 @@
             kind, (2, 6)[way], rs_end.at[kind, slot], end_recv.at[kind, slot], device, *more
         )
 
+    final = fin[0]
+    self_probs = self_e[...] * (jnp.exp2(own_high - final[0:1]) * final[1:2])
+    self_slopes = (self_probs * (self_p[...] - final[2:3])).astype(BF16)
+    self_keys = ck_ref[...].astype(F32).T.astype(BF16)
+    dq_self[...] = (jnp.dot(self_keys, self_slopes, preferred_element_type=F32) * SCALING).T
     for kind, way in ((1, 0), (0, 1), (0, 0), (1, 1)):
         two_on(kind, way)
     second_pass(0, 0)
 
-    grads = dq_self[pl.ds(pl.multiple_of(core * ROWS, ROWS), ROWS)] + dq_sum[0].astype(F32)
+    grads = dq_self[pl.ds(pl.multiple_of(core * ROWS, ROWS), ROWS)] + dq_out[core, 0].astype(F32)
     for r in NEAREST:
         arrived(dq_in.at[r], dq_send.at[1], dq_recv.at[r])
         grads += dq_in[r].astype(F32)
@@ -447,6 +467,11 @@
         out[...] = total.astype(BF16)
     for copy in sent:
         copy.wait_send()
+
+    @pl.when(core == 1)
+    def _():
+        for copy in final_sends():
+            copy.wait_send()
 
 
 def store(*refs):
@@ -491,15 +516,15 @@
             pltpu.VMEM((TILES, len(GROUPS), TILE), F32),
             pltpu.VMEM((TILES, 2, TILE), F32),
             pltpu.VMEM((TILES, 2, HD, TILE), F32),
+            pltpu.VMEM((TILES, 2, HD, TILE), F32),
             pltpu.VMEM((CHIPS, 4, 2 * ROWS), F32),
             pltpu.VMEM((PEERS, 4, 2 * ROWS), F32),
+            pltpu.VMEM((CHIPS, 4, 2 * ROWS), F32),
             pltpu.VMEM((4, 2 * ROWS), F32),
             pltpu.VMEM((CHIPS, 4, 2 * ROWS), F32),
             pltpu.VMEM((block, 2 * ROWS), F32),
             pltpu.VMEM((block, 2 * ROWS), F32),
             pltpu.VMEM((2, CHIPS, ROWS, HD), BF16),
-            pltpu.VMEM((CHIPS, ROWS, HD), BF16),
-            pltpu.VMEM((CHIPS, ROWS, HD), BF16),
             pltpu.VMEM((CHIPS, ROWS, HD), BF16),
             pltpu.VMEM((2 * ROWS, HD), F32),
             pltpu.VMEM((NZ, 2, KEYS, HD), F32),
@@ -511,12 +536,14 @@
             sem((PEERS,)),
             sem((2, NZ)),
             sem((2, NZ)),
+            sem((CHIPS,)),
             sem((PEERS,)),
             sem((PEERS,)),
             sem((CHIPS,)),
-            sem((CHIPS,)),
             sem,
             sem,
+            sem((TILES,)),
+            sem((TILES,)),
             sem((CHIPS,)),
             sem((CHIPS,)),
             sem((2, NZ)),

time: 46.6 us -> 45.5 us (0.976)
  Pallas kernels: 45.8 us -> 44.8 us
    pallas_call x1, Pallas kernels: 45.2 us -> 44.1 us  [body(): pl.pallas_call(kernel, out_shape=(pltpu.VMEM(queries.shape, BF16), pltpu....]
where the time goes in v5:
time: 45.5 us; the launch traced here: 45.4 us
  Pallas kernels  44.8 us (98%)
  between operations  0.64 us (1%)
    pallas_call x1, Pallas kernels, body(): pl.pallas_call(kernel, out_shape=(pltpu.VMEM(queries.shape, BF16), pltpu....  44.1 us

profile of v5, /device:TPU:1, one launch (start us, length us, event | category | flops | bytes accessed | tf_op | source)
XLA Modules:
  0.0 45.4 jit_solution(17391076703350508713)
XLA Ops:
  0.6 44.1 %attention_grads.1 = (bf16[8,1024]{1,0:T(8,128)(2,1)S(1)}, bf16[128,128]{1,0:T(8,128)(2,1)S(1)}, bf16[128,128]{1,0:T(8,128)(2,1)S(1)}) custom-call(bf16[8,1024]{1,0:T(8,128)(2,1)} %q_hbm.1, bf16[8,1024]{1,0:T(8,128)(2,1)} %g_hbm.1, bf16[128,128]{1,0:T(8,128)(2,1)} %pk_hbm.1, bf16[128,128]{1,0:T(8,128)(2,1)} %pv_hbm.1, bf16[256,128]{1,0:T(8,128)(2,1)} %ck_hbm.1, ...), custom_call_target="tpu_custom_call" | custom-call | tf_op jit(solution)/shard_map/attention_grads/pallas_call | solution.py:492
  44.8 0.7 %store.1 = (bf16[8,1024]{1,0:T(8,128)(2,1)}, bf16[128,128]{1,0:T(8,128)(2,1)}, bf16[128,128]{1,0:T(8,128)(2,1)}) custom-call(bf16[8,1024]{1,0:T(8,128)(2,1)S(1)} %get-tuple-element.6.refs_0_, bf16[128,128]{1,0:T(8,128)(2,1)S(1)} %get-tuple-element.7.refs_1_, bf16[128,128]{1,0:T(8,128)(2,1)S(1)} %get-tuple-element.8.refs_2_), custom_call_target="tpu_custom_call" | custom-call | tf_op jit(solution)/shard_map/store/pallas_call | solution.py:559

commit v6 on v5

--- a/solution.py
+++ b/solution.py
@@ -277,16 +277,16 @@
         for back in (3, 5, 4):
             kv_wait(kind, back)
     run_first_pass(0, 3, (2,))
+    lax.fori_loop(0, 3, close_rows, 0)
     for first, second in ((3, 1), (3, 2), (1, 3), (2, 3), (3, 3)):
         rows_from(first, second)
 
     def last_tiles(t, carry):
         tile_wait((t,))
         first_pass(t, (0, 1, 2))
-        return carry
+        return close_rows(t, carry)
 
     lax.fori_loop(3, TILES, last_tiles, 0)
-    lax.fori_loop(0, TILES, close_rows, 0)
 
     send(stat_out, stat_mate, mate_send, mate_recv, mate)
     for r in FARTHEST:
@@ -363,23 +363,21 @@
     def _():
         arrived(fin.at[0], fin_send.at[0], fin_recv.at[0])
 
-    for t in range(TILES):
-        remote(ab.at[t], ab_mate.at[t], ab_send.at[t], ab_recv.at[t], mate).wait()
-    for r in NEAREST:
-        arrived(fin.at[r], fin_send.at[1], fin_recv.at[r])
+    def final_wait(chips_there):
+        for r in chips_there:
+            arrived(fin.at[r], fin_send.at[1], fin_recv.at[r])
 
     def close_weights(t, carry):
         final = jnp.concatenate([fin[2 * t], fin[2 * t + 1]], axis=1)
         mg[t] = jnp.exp2(mg[t] - final[0:1]) * final[1:2]
         return carry
 
-    lax.fori_loop(0, TILES, close_weights, 0)
-
-    def second_pass(place, carry):
+
+    def second_pass(place, carry, tiles=range(TILES), more=False):
         g = lax.div(place + 1, 3)
         grad_k = jnp.zeros((KEYS, HD), F32)
         grad_v = jnp.zeros((KEYS, HD), F32)
-        for t in range(TILES):
+        for t in tiles:
             delta = jnp.concatenate([fin[2 * t, 2:3], fin[2 * t + 1, 2:3]], axis=1)
             at = pl.ds(pl.multiple_of(place * KEYS, KEYS), KEYS)
             probs = e_buf[t, at] * mg[t, pl.ds(g, 1)]
@@ -388,8 +386,9 @@
             rows_g = qg[4 * t : 4 * t + 4, ROWS : 2 * ROWS].reshape(TILE, HD)
             grad_v += jnp.dot(probs.astype(BF16), rows_g, preferred_element_type=F32)
             grad_k += jnp.dot(slopes, rows_q, preferred_element_type=F32)
-        part[place, 0] = grad_k * SCALING
-        part[place, 1] = grad_v
+        grad_k = grad_k * SCALING
+        part[place, 0] = part[place, 0] + grad_k if more else grad_k
+        part[place, 1] = part[place, 1] + grad_v if more else grad_v
         return carry
 
     def pass_on(kind, back, dst, sem, device, *more):
@@ -400,13 +399,19 @@
         rs_out[kind, at] = total.astype(BF16)
         send(rs_out.at[kind, at], dst, rs_send.at[kind, at], sem, device)
 
-    second_pass(PLACE[4], 0)
+    near_tiles, far_tiles = range(TILES // 2), range(TILES // 2, TILES)
+    final_wait(range(1, CHIPS // 2))
+    lax.fori_loop(0, TILES // 2, close_weights, 0)
+    lax.fori_loop(0, 3, lambda i, c: second_pass(7 - i, c, near_tiles), 0)
+    final_wait(range(CHIPS // 2, CHIPS))
+    lax.fori_loop(TILES // 2, TILES, close_weights, 0)
+    second_pass(PLACE[4], 0, far_tiles, True)
     pass_on(0, 4, rs_far.at[0], far_recv.at[0], down2)
     pass_on(1, 4, rs_far.at[1], far_recv.at[1], up2)
-    second_pass(PLACE[3], 0)
+    second_pass(PLACE[3], 0, far_tiles, True)
     for kind in range(2):
         pass_on(kind, 3, rs_near.at[kind, 0], near_recv.at[kind, 0], down)
-    second_pass(PLACE[5], 0)
+    second_pass(PLACE[5], 0, far_tiles, True)
     for kind in range(2):
         pass_on(kind, 5, rs_near.at[kind, 1], near_recv.at[kind, 1], up)
 
@@ -422,6 +427,8 @@
                 dq_out[c, 2 * t + i] = rows[at : at + ROWS]
         return carry
 
+    for t in range(TILES):
+        remote(ab.at[t], ab_mate.at[t], ab_send.at[t], ab_recv.at[t], mate).wait()
     lax.fori_loop(0, TILES, query_pass, 0)
     for r in FARTHEST:
         send(dq_out.at[core, r], dq_in.at[SEEN[r]], dq_send.at[r], dq_recv.at[SEEN[r]], chips[r])

time: 45.5 us -> 45.2 us (level)
  no operation moved by 1% of the time
where the time goes in v6:
time: 45.2 us; the launch traced here: 45.1 us
  Pallas kernels  44.5 us (98%)
  between operations  0.64 us (1%)
    pallas_call x1, Pallas kernels, body(): pl.pallas_call(kernel, out_shape=(pltpu.VMEM(queries.shape, BF16), pltpu....  43.8 us

profile of v6, /device:TPU:1, one launch (start us, length us, event | category | flops | bytes accessed | tf_op | source)
XLA Modules:
  0.0 45.1 jit_solution(7859912841167291847)
XLA Ops:
  0.6 43.8 %attention_grads.1 = (bf16[8,1024]{1,0:T(8,128)(2,1)S(1)}, bf16[128,128]{1,0:T(8,128)(2,1)S(1)}, bf16[128,128]{1,0:T(8,128)(2,1)S(1)}) custom-call(bf16[8,1024]{1,0:T(8,128)(2,1)} %q_hbm.1, bf16[8,1024]{1,0:T(8,128)(2,1)} %g_hbm.1, bf16[128,128]{1,0:T(8,128)(2,1)} %pk_hbm.1, bf16[128,128]{1,0:T(8,128)(2,1)} %pv_hbm.1, bf16[256,128]{1,0:T(8,128)(2,1)} %ck_hbm.1, ...), custom_call_target="tpu_custom_call" | custom-call | tf_op jit(solution)/shard_map/attention_grads/pallas_call | solution.py:499
  44.5 0.7 %store.1 = (bf16[8,1024]{1,0:T(8,128)(2,1)}, bf16[128,128]{1,0:T(8,128)(2,1)}, bf16[128,128]{1,0:T(8,128)(2,1)}) custom-call(bf16[8,1024]{1,0:T(8,128)(2,1)S(1)} %get-tuple-element.6.refs_0_, bf16[128,128]{1,0:T(8,128)(2,1)S(1)} %get-tuple-element.7.refs_1_, bf16[128,128]{1,0:T(8,128)(2,1)S(1)} %get-tuple-element.8.refs_2_), custom_call_target="tpu_custom_call" | custom-call | tf_op jit(solution)/shard_map/store/pallas_call | solution.py:566

commit v7 on v6

--- a/solution.py
+++ b/solution.py
@@ -269,10 +269,10 @@
     for kind in range(2):
         for back in (1, 7):
             kv_wait(kind, back)
+    for first, second in ((1, 1), (2, 1), (1, 2), (2, 2)):
+        rows_from(first, second)
     tile_wait((0, 1, 2))
     run_first_pass(0, 3, (0, 1))
-    for first, second in ((1, 1), (2, 1), (1, 2), (2, 2)):
-        rows_from(first, second)
     for kind in range(2):
         for back in (3, 5, 4):
             kv_wait(kind, back)

time: 45.2 us -> 45.7 us (1.011)
  no operation moved by 1% of the time
where the time goes in v7:
time: 45.7 us; the launch traced here: 45.5 us
  Pallas kernels  44.9 us (98%)
  between operations  0.64 us (1%)
    pallas_call x1, Pallas kernels, body(): pl.pallas_call(kernel, out_shape=(pltpu.VMEM(queries.shape, BF16), pltpu....  44.2 us

profile of v7, /device:TPU:1, one launch (start us, length us, event | category | flops | bytes accessed | tf_op | source)
XLA Modules:
  0.0 45.5 jit_solution(4215269606846940496)
XLA Ops:
  0.6 44.2 %attention_grads.1 = (bf16[8,1024]{1,0:T(8,128)(2,1)S(1)}, bf16[128,128]{1,0:T(8,128)(2,1)S(1)}, bf16[128,128]{1,0:T(8,128)(2,1)S(1)}) custom-call(bf16[8,1024]{1,0:T(8,128)(2,1)} %q_hbm.1, bf16[8,1024]{1,0:T(8,128)(2,1)} %g_hbm.1, bf16[128,128]{1,0:T(8,128)(2,1)} %pk_hbm.1, bf16[128,128]{1,0:T(8,128)(2,1)} %pv_hbm.1, bf16[256,128]{1,0:T(8,128)(2,1)} %ck_hbm.1, ...), custom_call_target="tpu_custom_call" | custom-call | tf_op jit(solution)/shard_map/attention_grads/pallas_call | solution.py:499
  44.9 0.7 %store.1 = (bf16[8,1024]{1,0:T(8,128)(2,1)}, bf16[128,128]{1,0:T(8,128)(2,1)}, bf16[128,128]{1,0:T(8,128)(2,1)}) custom-call(bf16[8,1024]{1,0:T(8,128)(2,1)S(1)} %get-tuple-element.6.refs_0_, bf16[128,128]{1,0:T(8,128)(2,1)S(1)} %get-tuple-element.7.refs_1_, bf16[128,128]{1,0:T(8,128)(2,1)S(1)} %get-tuple-element.8.refs_2_), custom_call_target="tpu_custom_call" | custom-call | tf_op jit(solution)/shard_map/store/pallas_call | solution.py:566
